TPU v7x, 128 devices: a whole 4x4x4 slice. The times are simulated.
128 devices in a mesh: ep: 32 (over z, x, core), dp: 4 (over y).
Axes of the slice: x: 4, y: 4, z: 4, core: 2. Of those that a mesh axis runs over, the one named last changes fastest.
Arguments:
- residual: bfloat16 [16384, 2880], P(('ep', 'dp')), may hold values from -400 to 400, as said below
- norm_gain: float32 [2880], replicated, may hold values from 0.25 to 1.75
- router_weight: bfloat16 [2880, 128], replicated, may hold values from -0.109375 to 0.109375
- out_grad: bfloat16 [16384, 2880], P(('ep', 'dp')), may hold values from -6 to 6
- expert_ids: int32 [16384, 4], P(('ep', 'dp')), may hold values from 0 to 127, all different within a row; in each aligned block of 128 rows (0 to 127, 128 to 255, ...) at most 6 rows name the same one
- hidden: bfloat16 [128, 768, 1440], P(('ep', 'dp')), may hold values from -0.3125 to 0.3125
- down_weight: bfloat16 [128, 1440, 2880], P(('ep', 'dp')), may hold values from -0.15625 to 0.15625
Outputs:
- hidden_grad: bfloat16 [128, 768, 1440], P(('ep', 'dp'))
- down_weight_grad: bfloat16 [128, 1440, 2880], P(('ep', 'dp'))
- residual_grad: bfloat16 [16384, 2880], P(('ep', 'dp'))
- router_grad: float32 [2880, 128], replicated
- gain_grad: float32 [2880], replicated
Inputs may be any that keep to these rules, and one draw needn't show every extreme that they name: `expert_ids`: in the tokens of one device no expert is named more than 6 times, a bound that some block reaches. `residual`: Real-valued entries.
All inputs are finite; a program needn't handle non-finite values.
Results may differ from a plain program's by a relative error of at most 0.0085.
Values may be sent and summed in bfloat16 or wider, within the bound.
A program may use at most 128 MiB of HBM per device.

v0:
```python
import jax
import jax.numpy as jnp
from jax import lax
from jax.sharding import Mesh
from jax.sharding import PartitionSpec as P

EP = ("ep_0", "ep_1", "ep_2")
EP_DP = ("ep_0", "ep_1", "ep_2", "dp")


def side_by_side(arrays, axis, split_dim, concat_dim, along):
    columns = [a.reshape(*a.shape[:along], -1) for a in arrays]
    both = jnp.concatenate(columns, axis=along)
    whole, at, finished = (
        lax.all_to_all(both, axis, split_axis=split_dim, concat_axis=concat_dim, tiled=True),
        0,
        [],
    )
    for a, column in zip(arrays, columns):
        slab = whole[..., at : at + column.shape[along]]
        finished.append(slab.reshape(*slab.shape[:along], *a.shape[along:]))
        at += column.shape[along]
    return tuple(finished)


def in_blocks(shard, dim, size):
    before, after = (shard.shape[:dim], shard.shape[dim + 1 :])
    return jnp.moveaxis(shard.reshape(*before, size, -1, *after), dim, 0)


def in_order(pieces, dim):
    pieces = jnp.moveaxis(pieces, 0, dim)
    lengths = pieces.shape
    return pieces.reshape(*lengths[:dim], lengths[dim] * lengths[dim + 1], *lengths[dim + 2 :])


def joined_exchange(shard, axis, axes, splits, concats):
    sizes = [lax.axis_size(a) for a in axes]
    pieces = in_blocks(shard, splits[0], sizes[0])
    pieces = jnp.moveaxis(in_blocks(pieces, splits[1] + 1, sizes[1]), 0, 1)
    inside = pieces.shape[2:]
    pieces = pieces.reshape(-1, *inside)
    pieces = lax.all_to_all(pieces, axis, split_axis=0, concat_axis=0, tiled=True)
    pieces = in_order(pieces.reshape(*sizes, *inside), concats[0] + 1)
    return in_order(pieces, concats[1])


def rows_for(lines, size):
    spare = -len(lines) % size
    return jnp.pad(lines, [(0, spare)] + [(0, 0)] * (lines.ndim - 1))


def sent_to_all(shard, axis):
    size = lax.axis_size(axis)
    return lax.all_to_all(
        jnp.broadcast_to(shard[None], (size, *shard.shape)), axis, 0, 0, tiled=True
    )


def gathered_by_axis(shard, axes, dim):
    far, near = axes
    first = sent_to_all(shard, far)
    pieces = jnp.swapaxes(sent_to_all(first, near), 0, 1)
    return in_order(pieces.reshape(-1, *shard.shape), dim)


def summed_on_arrival(shard, axis, dim):
    size = lax.axis_size(axis)
    pieces = lax.all_to_all(in_blocks(shard, dim, size), axis, 0, 0, tiled=True)
    return jnp.sum(pieces.astype(jnp.float32), axis=0)


def sum_by_axis(shard, axes, dim):
    far, near = axes
    pieces = in_blocks(shard, dim, lax.axis_size(far))
    nearer = summed_on_arrival(pieces, near, dim + 1)
    arrived = lax.all_to_all(
        nearer.astype(jnp.bfloat16), far, split_axis=0, concat_axis=0, tiled=True
    )
    return arrived.astype(jnp.float32).sum(axis=0)


def nested_sum(shard, axes):
    lines = shard.reshape(-1)
    padded = rows_for(lines, lax.axis_size(axes[0]) * lax.axis_size(axes[1]))
    whole = gathered_by_axis(sum_by_axis(padded, axes, 0).astype(jnp.bfloat16), axes, 0)
    return lax.slice_in_dim(whole, 0, len(lines)).reshape(shard.shape).astype(jnp.float32)


def on_device(residual, norm_gain, router_weight, out_grad, expert_ids, hidden, down_weight):
    tokens_here, width = residual.shape
    top_count = expert_ids.shape[1]
    experts = router_weight.shape[1]
    slots = hidden.shape[1]
    capacity = slots // experts
    ep_count = lax.axis_size(EP)
    dp_count = lax.axis_size("dp")
    floated = residual.astype(jnp.float32)
    inverse = lax.rsqrt(jnp.mean(floated * floated, -1, keepdims=True) + 1e-05)
    unit = floated * inverse
    normed = (unit * norm_gain).astype(jnp.bfloat16)
    logits = jnp.dot(normed, router_weight, preferred_element_type=jnp.float32)
    match = expert_ids[:, :, None] == jnp.arange(experts, dtype=jnp.int32)[None, None, :]
    picked = jnp.sum(jnp.where(match, logits[:, None, :], jnp.float32(0.0)), -1)
    expo = jnp.exp(picked)
    prob = expo / jnp.sum(expo, -1, keepdims=True)
    flat_ids = expert_ids.reshape(-1)
    onehot = (flat_ids[:, None] == jnp.arange(experts, dtype=jnp.int32)[None, :]).astype(jnp.int32)
    slot_rank = jnp.sum((jnp.cumsum(onehot, 0) - onehot) * onehot, -1)
    place = flat_ids * capacity + slot_rank
    repeated = jnp.repeat(out_grad, top_count, axis=0)
    send_rows = jnp.zeros((experts * capacity, width), jnp.bfloat16).at[place].set(repeated)
    send_prob = (
        jnp.zeros((experts * capacity,), jnp.bfloat16)
        .at[place]
        .set(prob.astype(jnp.bfloat16).reshape(-1))
    )
    got_rows, got_prob = side_by_side((send_rows, send_prob), EP_DP, 0, 0, 1)
    hidden_rows = hidden[0]
    weight = down_weight[0]
    inner = lax.dot_general(
        got_rows, weight, (((1,), (1,)), ((), ())), preferred_element_type=jnp.float32
    )
    slot_score = jnp.sum(inner * hidden_rows.astype(jnp.float32), -1)
    weight_col = got_prob.astype(jnp.float32)[:, None]
    hidden_grad = (weight_col * inner).astype(jnp.bfloat16)
    scaled = (weight_col * got_rows.astype(jnp.float32)).astype(jnp.bfloat16)
    weight_grad = lax.dot_general(
        hidden_rows, scaled, (((0,), (0,)), ((), ())), preferred_element_type=jnp.float32
    )
    came_back = joined_exchange(
        slot_score.reshape(ep_count, dp_count * capacity), EP_DP, (EP, "dp"), (0, 1), (0, 1)
    ).reshape(-1)
    score = came_back[place].reshape(tokens_here, top_count)
    pick_grad = prob * (score - jnp.sum(prob * score, -1, keepdims=True))
    logit_grad = jnp.sum(jnp.where(match, pick_grad[:, :, None], jnp.float32(0.0)), 1)
    local_router = jnp.dot(
        normed.astype(jnp.float32).T, logit_grad, precision=lax.Precision.HIGHEST
    )
    normed_grad = jnp.dot(
        logit_grad, router_weight.astype(jnp.float32).T, precision=lax.Precision.HIGHEST
    )
    local_gain = jnp.sum(normed_grad * unit, 0)
    router_grad, gain_grad = (
        nested_sum(local_router.astype(jnp.bfloat16), (("ep_0", "ep_1"), ("ep_2", "dp"))),
        nested_sum(local_gain.astype(jnp.bfloat16), (("ep_0", "ep_1"), ("ep_2", "dp"))),
    )
    upper = normed_grad * norm_gain
    residual_grad = (inverse * (upper - unit * jnp.mean(upper * unit, -1, keepdims=True))).astype(
        jnp.bfloat16
    )
    return (
        hidden_grad[None],
        weight_grad.astype(jnp.bfloat16)[None],
        residual_grad,
        router_grad,
        gain_grad,
    )


def solution(mesh):
    finer = Mesh(mesh.devices.reshape(4, 4, 2, mesh.shape["dp"]), ("ep_0", "ep_1", "ep_2", "dp"))
    placed = (
        P(EP_DP, None),
        P(),
        P(),
        P(EP_DP, None),
        P(EP_DP, None),
        P(EP_DP, None, None),
        P(EP_DP, None, None),
    )
    return jax.shard_map(
        on_device,
        mesh=finer,
        in_specs=placed,
        out_specs=(P(EP_DP, None, None), P(EP_DP, None, None), P(EP_DP, None), P(), P()),
        check_vma=False,
    )
```

profile of v0, /device:TPU:1, one launch (start us, length us, event | category | flops | bytes accessed | tf_op | source)
XLA Modules:
  0.0 271.5 jit_solution(7505240279958353495)
XLA Ops:
  7.5 3.9 %scatter_custom_fusion.1 = bf16[768]{0:T(1024)(128)(2,1)S(1)} fusion(s32[512]{0:T(512)S(1)} %bitcast.69, bf16[512]{0:T(512)(128)(2,1)S(1)} %reshape.186, bf16[]{:T(256)} %constant.20.clone.1), kind=kCustom, calls=%fused_computation.58 | custom fusion | bytes 1538 | tf_op jit(solution)/shard_map/scatter | solution.py:116
  14.5 5.6 %reshape.178 = bf16[512,2880]{1,0:T(8,128)(2,1)} reshape(bf16[128,4,2880]{2,1,0:T(4,128)(2,1)} %broadcast_in_dim.45) | data formatting | bytes 5898240 | tf_op jit(solution)/shard_map/reshape | solution.py:111
  20.1 8.7 %scatter_custom_fusion = bf16[768,2880]{1,0:T(8,128)(2,1)} fusion(s32[512]{0:T(512)S(1)} %bitcast.70, bf16[512,2880]{1,0:T(8,128)(2,1)} %reshape.178, bf16[]{:T(256)} %constant.20.clone.1), kind=kCustom, calls=%fused_computation.15 | custom fusion | bytes 4424192 | tf_op jit(solution)/shard_map/scatter | solution.py:112
  28.9 7.5 %concatenate.8 = bf16[128,6,2880]{2,1,0:T(8,128)(2,1)} reshape(bf16[768,2880]{1,0:T(8,128)(2,1)} %scatter_custom_fusion) | data formatting | bytes 8847360 | tf_op jit(solution)/shard_map/concatenate | solution.py:13
  36.4 3.9 %pad_maximum_fusion = bf16[128,6,2881]{2,1,0:T(8,128)(2,1)S(1)} fusion(bf16[128,6,1]{2,1,0:T(8,128)(2,1)S(1)} %concatenate.11, bf16[128,6,2880]{2,1,0:T(8,128)(2,1)} %concatenate.8), kind=kLoop, calls=%fused_computation.8 | loop fusion | flops 8850432 | bytes 8850432 | tf_op jit(solution)/shard_map/concatenate | solution.py:13
  40.3 84.1 %all_to_all.64 = bf16[128,6,2881]{2,1,0:T(8,128)(2,1)} all-to-all(bf16[128,6,2881]{2,1,0:T(8,128)(2,1)S(1)} %pad_maximum_fusion), channel_id=1, replica_groups=mesh['ep_0'=4,'ep_1'=4,'ep_2'=2,'dp'=4] {'ep_0','ep_1','ep_2','dp'}, dimensions={0} | all-to-all | bytes 8850432 | tf_op jit(solution)/shard_map/all_to_all | solution.py:15
  124.4 8.2 %all_to_all.42 = bf16[768,2881]{1,0:T(8,128)(2,1)} reshape(bf16[128,6,2881]{2,1,0:T(8,128)(2,1)} %all_to_all.64) | data formatting | bytes 8850432 | tf_op jit(solution)/shard_map/all_to_all | solution.py:15
  133.8 12.3 %multiply_reduce_fusion = (f32[768]{0:T(1024)S(1)}, bf16[1,768,1440]{1,2,0:T(8,128)(2,1)}) fusion(bf16[1,768,1440]{1,2,0:T(8,128)(2,1)} %param.12, f32[768]{0:T(1024)S(1)} %convert_reduce_fusion, bf16[1,1440,2880]{2,1,0:T(8,128)(2,1)} %param.13, bf16[768,2881]{1,0:T(8,128)(2,1)} %all_to_all.42), kind=kOutput, calls=%fused_computation.10 | convolution fusion | flops 6375627776 | bytes 17149440 | tf_op jit(solution)/shard_map/dot_general | solution.py:121
  146.8 3.8 %all-to-all-start.1 = ((f32[128,1,6]{2,1,0:T(1,128)}), f32[128,1,6]{2,1,0:T(1,128)S(1)}, u32[]{:S(2)}, u32[]{:S(2)}) async-start(f32[128,1,6]{2,1,0:T(1,128)} %bitcast.10), calls=%async_computation.1 | async-start | bytes 131072 | tf_op jit(solution)/shard_map/all_to_all | solution.py:43
  150.7 9.6 %all-to-all-done.1 = f32[128,1,6]{2,1,0:T(1,128)S(1)} async-done(((f32[128,1,6]{2,1,0:T(1,128)}), f32[128,1,6]{2,1,0:T(1,128)S(1)}, u32[]{:S(2)}, u32[]{:S(2)}) %all-to-all-start.1) | async-done | bytes 3104 | tf_op jit(solution)/shard_map/all_to_all | solution.py:43
  165.2 4.0 %all-to-all-start.6 = ((bf16[8,2,184]{2,1,0:T(2,128)(2,1)}), bf16[8,2,184]{2,1,0:T(2,128)(2,1)S(1)}, u32[]{:S(2)}, u32[]{:S(2)}) async-start(bf16[8,2,184]{2,1,0:T(2,128)(2,1)} %reshape.199), calls=%async_computation.6 | async-start | bytes 16384 | tf_op jit(solution)/shard_map/all_to_all | solution.py:69
  175.4 4.8 %all-to-all-start.2 = ((bf16[8,16,2880]{2,1,0:T(8,128)(2,1)}), bf16[8,16,2880]{2,1,0:T(8,128)(2,1)}, u32[]{:S(2)}, u32[]{:S(2)}) async-start(bf16[8,16,2880]{2,1,0:T(8,128)(2,1)} %bitcast.57), calls=%async_computation.2 | async-start | bytes 1507328 | tf_op jit(solution)/shard_map/all_to_all | solution.py:69
  181.0 11.2 %all-to-all-done.2 = bf16[8,16,2880]{2,1,0:T(8,128)(2,1)} async-done(((bf16[8,16,2880]{2,1,0:T(8,128)(2,1)}), bf16[8,16,2880]{2,1,0:T(8,128)(2,1)}, u32[]{:S(2)}, u32[]{:S(2)}) %all-to-all-start.2) | async-done | bytes 737312 | tf_op jit(solution)/shard_map/all_to_all | solution.py:69
  192.1 3.5 %all-to-all-start.7 = ((bf16[16,1,23]{2,1,0:T(2,128)(2,1)}), bf16[16,1,23]{2,1,0:T(2,128)(2,1)S(1)}, u32[]{:S(2)}, u32[]{:S(2)}) async-start(bf16[16,1,23]{2,1,0:T(2,128)(2,1)} %copy.63), calls=%async_computation.7 | async-start | bytes 16384 | tf_op jit(solution)/shard_map/all_to_all | solution.py:77
  201.9 3.5 %all-to-all-start.3 = ((bf16[16,2,1440]{2,1,0:T(2,128)(2,1)}), bf16[16,2,1440]{2,1,0:T(2,128)(2,1)S(1)}, u32[]{:S(2)}, u32[]{:S(2)}) async-start(bf16[16,2,1440]{2,1,0:T(2,128)(2,1)} %reshape.195), calls=%async_computation.3 | async-start | bytes 196608 | tf_op jit(solution)/shard_map/all_to_all | solution.py:77
  205.5 6.6 %all-to-all-done.3 = bf16[16,2,1440]{2,1,0:T(2,128)(2,1)S(1)} async-done(((bf16[16,2,1440]{2,1,0:T(2,128)(2,1)}), bf16[16,2,1440]{2,1,0:T(2,128)(2,1)S(1)}, u32[]{:S(2)}, u32[]{:S(2)}) %all-to-all-start.3) | async-done | bytes 92192 | tf_op jit(solution)/shard_map/all_to_all | solution.py:77
  212.7 3.5 %all-to-all-start.8 = ((bf16[16,1,23]{2,1,0:T(2,128)(2,1)}), bf16[16,1,23]{2,1,0:T(2,128)(2,1)S(1)}, u32[]{:S(2)}, u32[]{:S(2)}) async-start(bf16[16,1,23]{2,1,0:T(2,128)(2,1)} %broadcast_in_dim.91), calls=%async_computation.8 | async-start | bytes 16384 | tf_op jit(solution)/shard_map/all_to_all | solution.py:55
  218.7 3.8 %all-to-all-done.8 = bf16[16,1,23]{2,1,0:T(2,128)(2,1)S(1)} async-done(((bf16[16,1,23]{2,1,0:T(2,128)(2,1)}), bf16[16,1,23]{2,1,0:T(2,128)(2,1)S(1)}, u32[]{:S(2)}, u32[]{:S(2)}) %all-to-all-start.8) | async-done | bytes 768 | tf_op jit(solution)/shard_map/all_to_all | solution.py:55
  222.5 3.5 %all-to-all-start.4 = ((bf16[16,2,1440]{2,1,0:T(2,128)(2,1)}), bf16[16,2,1440]{2,1,0:T(2,128)(2,1)S(1)}, u32[]{:S(2)}, u32[]{:S(2)}) async-start(bf16[16,2,1440]{2,1,0:T(2,128)(2,1)} %reshape.197), calls=%async_computation.4 | async-start | bytes 196608 | tf_op jit(solution)/shard_map/all_to_all | solution.py:55
  226.0 12.1 %fusion = bf16[1,1440,2880]{2,1,0:T(8,128)(2,1)} fusion(f32[768]{0:T(1024)S(1)} %convert_reduce_fusion, bf16[768,2881]{1,0:T(8,128)(2,1)} %all_to_all.42, bf16[1,768,1440]{1,2,0:T(8,128)(2,1)} %param.12), kind=kOutput, calls=%fused_computation.4 | convolution fusion | flops 6380881920 | bytes 14934528 | tf_op jit(solution)/shard_map/dot_general | solution.py:128
  238.8 6.9 %all-to-all-start.9 = ((bf16[8,2,184]{2,1,0:T(2,128)(2,1)}), bf16[8,2,184]{2,1,0:T(2,128)(2,1)S(1)}, u32[]{:S(2)}, u32[]{:S(2)}) async-start(bf16[8,2,184]{2,1,0:T(2,128)(2,1)} %reshape.201), calls=%async_computation.9 | async-start | bytes 16384 | tf_op jit(solution)/shard_map/all_to_all | solution.py:55
  245.9 4.7 %all-to-all-done.9 = bf16[8,2,184]{2,1,0:T(2,128)(2,1)S(1)} async-done(((bf16[8,2,184]{2,1,0:T(2,128)(2,1)}), bf16[8,2,184]{2,1,0:T(2,128)(2,1)S(1)}, u32[]{:S(2)}, u32[]{:S(2)}) %all-to-all-start.9) | async-done | bytes 5920 | tf_op jit(solution)/shard_map/all_to_all | solution.py:55
  251.5 4.5 %all-to-all-start.5 = ((bf16[8,16,2880]{2,1,0:T(8,128)(2,1)}), bf16[8,16,2880]{2,1,0:T(8,128)(2,1)}, u32[]{:S(2)}, u32[]{:S(2)}) async-start(bf16[8,16,2880]{2,1,0:T(8,128)(2,1)} %broadcast_in_dim.90), calls=%async_computation.5 | async-start | bytes 1507328 | tf_op jit(solution)/shard_map/all_to_all | solution.py:55
  258.3 9.7 %all-to-all-done.5 = bf16[8,16,2880]{2,1,0:T(8,128)(2,1)} async-done(((bf16[8,16,2880]{2,1,0:T(8,128)(2,1)}), bf16[8,16,2880]{2,1,0:T(8,128)(2,1)}, u32[]{:S(2)}, u32[]{:S(2)}) %all-to-all-start.5) | async-done | bytes 737312 | tf_op jit(solution)/shard_map/all_to_all | solution.py:55
  (87 shorter events, 40.6 us)
Async XLA Ops:
  0.6 4.0 %copy-start = (bf16[2880,128]{1,0:T(8,128)(2,1)S(1)}, bf16[2880,128]{1,0:T(8,128)(2,1)}, u32[]{:S(2)}) copy-start(bf16[2880,128]{1,0:T(8,128)(2,1)} %param.9) | copy-start | bytes 2211844
  0.6 6.1 %copy-start.4 = (s32[128,4]{0,1:T(4,128)S(1)}, s32[128,4]{0,1:T(4,128)}, u32[]{:S(2)}) copy-start(s32[128,4]{0,1:T(4,128)} %param.11) | copy-start | bytes 6148
  0.7 11.1 %copy-start.2 = (bf16[128,2880]{0,1:T(8,128)(2,1)S(1)}, bf16[128,2880]{0,1:T(8,128)(2,1)}, u32[]{:S(2)}) copy-start(bf16[128,2880]{0,1:T(8,128)(2,1)} %param.10) | copy-start | bytes 2211844
  133.8 29.4 %copy-start.1 = (bf16[128,2880]{0,1:T(8,128)(2,1)S(1)}, bf16[128,2880]{0,1:T(8,128)(2,1)}, u32[]{:S(2)}) copy-start(bf16[128,2880]{0,1:T(8,128)(2,1)} %param.7) | copy-start | bytes 2211844
  133.8 29.4 %copy-start.3 = (f32[2880]{0:T(1024)S(1)}, f32[2880]{0:T(1024)}, u32[]{:S(2)}) copy-start(f32[2880]{0:T(1024)} %param.8) | copy-start | bytes 34564
  146.8 13.4 %all-to-all-start.1 = ((f32[128,1,6]{2,1,0:T(1,128)}), f32[128,1,6]{2,1,0:T(1,128)S(1)}, u32[]{:S(2)}, u32[]{:S(2)}) async-start(f32[128,1,6]{2,1,0:T(1,128)} %bitcast.10), calls=%async_computation.1 | async-start | bytes 131072 | tf_op jit(solution)/shard_map/all_to_all | solution.py:43
  165.2 10.3 %all-to-all-start.6 = ((bf16[8,2,184]{2,1,0:T(2,128)(2,1)}), bf16[8,2,184]{2,1,0:T(2,128)(2,1)S(1)}, u32[]{:S(2)}, u32[]{:S(2)}) async-start(bf16[8,2,184]{2,1,0:T(2,128)(2,1)} %reshape.199), calls=%async_computation.6 | async-start | bytes 16384 | tf_op jit(solution)/shard_map/all_to_all | solution.py:69
  175.4 16.7 %all-to-all-start.2 = ((bf16[8,16,2880]{2,1,0:T(8,128)(2,1)}), bf16[8,16,2880]{2,1,0:T(8,128)(2,1)}, u32[]{:S(2)}, u32[]{:S(2)}) async-start(bf16[8,16,2880]{2,1,0:T(8,128)(2,1)} %bitcast.57), calls=%async_computation.2 | async-start | bytes 1507328 | tf_op jit(solution)/shard_map/all_to_all | solution.py:69
  192.1 9.8 %all-to-all-start.7 = ((bf16[16,1,23]{2,1,0:T(2,128)(2,1)}), bf16[16,1,23]{2,1,0:T(2,128)(2,1)S(1)}, u32[]{:S(2)}, u32[]{:S(2)}) async-start(bf16[16,1,23]{2,1,0:T(2,128)(2,1)} %copy.63), calls=%async_computation.7 | async-start | bytes 16384 | tf_op jit(solution)/shard_map/all_to_all | solution.py:77
  201.9 10.2 %all-to-all-start.3 = ((bf16[16,2,1440]{2,1,0:T(2,128)(2,1)}), bf16[16,2,1440]{2,1,0:T(2,128)(2,1)S(1)}, u32[]{:S(2)}, u32[]{:S(2)}) async-start(bf16[16,2,1440]{2,1,0:T(2,128)(2,1)} %reshape.195), calls=%async_computation.3 | async-start | bytes 196608 | tf_op jit(solution)/shard_map/all_to_all | solution.py:77
  212.7 9.8 %all-to-all-start.8 = ((bf16[16,1,23]{2,1,0:T(2,128)(2,1)}), bf16[16,1,23]{2,1,0:T(2,128)(2,1)S(1)}, u32[]{:S(2)}, u32[]{:S(2)}) async-start(bf16[16,1,23]{2,1,0:T(2,128)(2,1)} %broadcast_in_dim.91), calls=%async_computation.8 | async-start | bytes 16384 | tf_op jit(solution)/shard_map/all_to_all | solution.py:55
  222.5 16.3 %all-to-all-start.4 = ((bf16[16,2,1440]{2,1,0:T(2,128)(2,1)}), bf16[16,2,1440]{2,1,0:T(2,128)(2,1)S(1)}, u32[]{:S(2)}, u32[]{:S(2)}) async-start(bf16[16,2,1440]{2,1,0:T(2,128)(2,1)} %reshape.197), calls=%async_computation.4 | async-start | bytes 196608 | tf_op jit(solution)/shard_map/all_to_all | solution.py:55
  238.8 11.8 %all-to-all-start.9 = ((bf16[8,2,184]{2,1,0:T(2,128)(2,1)}), bf16[8,2,184]{2,1,0:T(2,128)(2,1)S(1)}, u32[]{:S(2)}, u32[]{:S(2)}) async-start(bf16[8,2,184]{2,1,0:T(2,128)(2,1)} %reshape.201), calls=%async_computation.9 | async-start | bytes 16384 | tf_op jit(solution)/shard_map/all_to_all | solution.py:55
  251.5 16.4 %all-to-all-start.5 = ((bf16[8,16,2880]{2,1,0:T(8,128)(2,1)}), bf16[8,16,2880]{2,1,0:T(8,128)(2,1)}, u32[]{:S(2)}, u32[]{:S(2)}) async-start(bf16[8,16,2880]{2,1,0:T(8,128)(2,1)} %broadcast_in_dim.90), calls=%async_computation.5 | async-start | bytes 1507328 | tf_op jit(solution)/shard_map/all_to_all | solution.py:55
where the time goes:
time: 273 us; the launch traced here: 272 us
  blocking collectives  84.1 us (31%)
  local copies, waits for them, and re-layouts  55.6 us (20%)
  waiting for transfers between devices  48.6 us (18%)
  starting transfers between devices  38 us (14%)
  matrix products  29.3 us (11%)
  other arithmetic  14.9 us (5%)
    all_to_all x1, blocking collectives, side_by_side(): lax.all_to_all(both, axis, split_axis=split_dim, concat_axis=concat_dim,...  84.1 us
    all_to_all x4, starting transfers between devices, sent_to_all(): lax.all_to_all(jnp.broadcast_to(shard[None], (size, *shard.shape)), axis,...  18.4 us
    all_to_all x4, waiting for transfers between devices, sent_to_all(): lax.all_to_all(jnp.broadcast_to(shard[None], (size, *shard.shape)), axis,...  18.2 us
    dot_general x1, matrix products, on_device(): lax.dot_general(got_rows, weight, (((1,), (1,)), ((), ())), preferred_ele...  12.3 us
    dot_general x1, matrix products, on_device(): lax.dot_general(hidden_rows, scaled, (((0,), (0,)), ((), ())), preferred_...  12.1 us
    all_to_all x2, waiting for transfers between devices, summed_on_arrival(): pieces = lax.all_to_all(in_blocks(shard, dim, size), axis, 0, 0, tiled=True)  11.2 us
    all_to_all x2, waiting for transfers between devices, sum_by_axis(): lax.all_to_all(nearer.astype(jnp.bfloat16), far, split_axis=0, concat_axi...  9.7 us
    all_to_all x1, waiting for transfers between devices, joined_exchange(): lax.all_to_all(pieces, axis, split_axis=0, concat_axis=0, tiled=True)  9.58 us
  transfers between devices with their start and end apart: 9, of which 7 were waited for; matrix products, arithmetic and copies ran while one was open for 10% of the time, Pallas kernels for 0%

commit v1 on v0

v1 whole, which is shorter than its diff:
```python
import functools

import jax
import jax.numpy as jnp
from jax import lax
from jax.experimental import pallas as pl
from jax.experimental.pallas import tpu as pltpu
from jax.sharding import Mesh
from jax.sharding import PartitionSpec as P

AX = ("ep_0", "ep_1", "ep_2", "dp")
SZ = (4, 4, 2, 4)
Z, X, CORE, Y = 0, 1, 2, 3
STRIDE = (32, 8, 4, 1)
MESH = pl.DeviceIdType.MESH
D = 2880
FF = 1440
BF = jnp.bfloat16
F32 = jnp.float32

PLAN = (
    (2560, 320, 384, Y, Z, X),
    (0, 512, 512, Y, X, Z),
    (512, 512, 512, Y, Z, X),
    (1024, 512, 512, Y, X, Z),
    (1536, 512, 512, Y, Z, X),
    (2048, 512, 512, Y, X, Z),
)
NCH = len(PLAN)
GDIMS = tuple(dict.fromkeys(c[3] for c in PLAN))
FBLK = ((0, 512), (512, 512), (1024, 416))
COLORS = ((Z, (X, CORE, Y)), (X, (Z, CORE, Y)), (Y, (Z, X, CORE)))
OTHER = {Z: (X, CORE, Y), X: (Z, CORE, Y), Y: (Z, X, CORE)}


def off(**kw):
    return kw


def plane_offsets(dims):
    out = []
    for a in range(SZ[dims[0]]):
        for b in range(SZ[dims[1]]):
            for c in range(SZ[dims[2]]):
                if (a, b, c) != (0, 0, 0):
                    t = [0, 0, 0, 0]
                    t[dims[0]], t[dims[1]], t[dims[2]] = a, b, c
                    out.append(tuple(t))
    return out


def spread(offsets):
    def hops(t):
        return sum(min(t[i], SZ[i] - t[i]) for i in (Z, X, Y))

    return sorted(offsets, key=lambda t: -hops(t))


def ring_offset(dim, d):
    t = [0, 0, 0, 0]
    t[dim] = d
    return tuple(t)


def all_peers():
    peers = []
    for c in PLAN:
        for d in (1, 2, 3):
            peers += [ring_offset(c[3], d), ring_offset(c[4], d)]
        for dq in range(4):
            for dc in range(2):
                if dq or dc:
                    t = [0, 0, 0, 0]
                    t[c[5]], t[CORE] = dq, dc
                    peers.append(tuple(t))
    peers += plane_offsets((Z, X, CORE))
    peers += [ring_offset(Y, d) for d in (1, 2, 3)]
    for a, others in COLORS:
        peers += [ring_offset(a, d) for d in (1, 2, 3)]
        peers += plane_offsets(others)
    return list(dict.fromkeys(peers))


PEERS = all_peers()


def inverse_of(t):
    return tuple((SZ[i] - t[i]) % SZ[i] for i in range(4))


def kernel(*refs):
    names = (
        ["og", "res", "gain", "rw", "ids", "hid_h", "w_h"]
        + ["hg_h", "sc_h", "rg", "tot"]
        + ["hid", "w", "acc", "hgs", "mt", "prob", "probb", "normed", "normedt", "unit"]
        + ["rsc", "rr", "xs", "ar1", "as2", "ar2", "gv", "rag"]
    )
    names += [f"mg{g}" for g in range(len(GDIMS))] + ["pg"] + [f"pb{g}" for g in range(len(GDIMS))]
    for i in range(NCH):
        names += [f"tok{i}", f"sb{i}", f"b1_{i}", f"fin{i}", f"scs{i}"]
    names += ["s_m", "r_m", "s_p", "r_p", "s_ag", "r_ag", "s_p1", "r_p1", "s_p2", "r_p2"]
    names += ["s_ret", "r_ret", "s_rety", "r_rety", "s_a1", "r_a1", "s_a2", "r_a2"]
    names += ["s_g2", "r_g2", "s_g1", "r_g1", "loc"]
    assert len(names) == len(refs)
    k = dict(zip(names, refs))
    me = [lax.axis_index(a) for a in AX]

    def dev(t):
        return tuple(
            lax.rem(me[i] + t[i], SZ[i]) if t[i] else me[i] for i in range(4)
        )

    def coord(dim, d):
        return lax.rem(me[dim] + d, SZ[dim]) if d else me[dim]

    def remote(src, dst, ssem, rsem, t):
        return pltpu.make_async_remote_copy(
            src_ref=src, dst_ref=dst, send_sem=ssem, recv_sem=rsem,
            device_id=dev(t), device_id_type=MESH,
        )

    pending = []

    def launch(src, dst, ssem, rsem, t):
        cp = remote(src, dst, ssem, rsem, t)
        cp.start()
        pending.append(cp)
        return cp

    barrier = pltpu.get_barrier_semaphore()
    for t in PEERS:
        pl.semaphore_signal(barrier, inc=1, device_id=dev(t), device_id_type=MESH)
    w_copy = pltpu.make_async_copy(k["w_h"], k["w"], k["loc"].at[0])
    w_copy.start()
    hid_copy = pltpu.make_async_copy(k["hid_h"], k["hid"], k["loc"].at[1])
    hid_copy.start()

    e_row = lax.broadcasted_iota(jnp.int32, (128, 128), 0)
    t_col = lax.broadcasted_iota(jnp.int32, (128, 128), 1)
    match = e_row == k["ids"][0:1, :]
    for j in range(1, 4):
        match = match | (e_row == k["ids"][j : j + 1, :])
    matchf = match.astype(F32)
    earlier = jnp.where(e_row < t_col, 1.0, 0.0).astype(BF)
    count = jnp.dot(matchf.astype(BF), earlier, preferred_element_type=F32)
    mt = matchf * (count + 1.0)
    k["mt"][...] = mt
    for g, a in enumerate(GDIMS):
        k[f"mg{g}"][me[a]] = mt.astype(BF)
    k["rag"][...] = jnp.zeros_like(k["rag"])
    k["rag"][:, 0:320] = k["og"][:, 2560:2880]
    pl.semaphore_wait(barrier, len(PEERS))

    m_cp = []
    for g, a in enumerate(GDIMS):
        own = k[f"mg{g}"].at[me[a]]
        m_cp.append([
            launch(own, own, k["s_m"].at[g, d - 1], k["r_m"].at[g, d - 1], ring_offset(a, d))
            for d in (2, 1, 3)
        ])
    ag = []
    for i, (c0, nc, cw, a, p, q) in enumerate(PLAN):
        src = k["rag"] if nc != cw else k["og"].at[:, pl.ds(c0, nc)]
        ag.append([
            launch(src, k[f"tok{i}"].at[me[a]], k["s_ag"].at[i, d - 1], k["r_ag"].at[i, d - 1], ring_offset(a, d))
            for d in (2, 1, 3)
        ])

    floated = k["res"][...].astype(F32)
    inv = lax.rsqrt(jnp.mean(floated * floated, -1, keepdims=True) + 1e-05)
    unit = floated * inv
    normed = (unit * k["gain"][...]).astype(BF)
    logits = jnp.dot(normed, k["rw"][...], preferred_element_type=F32)
    k["normed"][...] = normed
    expo = jnp.where(match, jnp.exp(logits.T), 0.0)
    prob = expo / jnp.sum(expo, 0, keepdims=True)
    k["prob"][...] = prob
    pa = PLAN[0][3]
    k["pg"][me[pa]] = prob.astype(BF)
    own = k["pg"].at[me[pa]]
    p_cp = [
        launch(own, own, k["s_p"].at[d - 1], k["r_p"].at[d - 1], ring_offset(pa, d)) for d in (2, 1, 3)
    ]
    for i, (c0, nc, cw, a, p, q) in enumerate(PLAN):
        k[f"tok{i}"][me[a]] = k["rag"][...] if nc != cw else k["og"][:, c0 : c0 + nc]

    group = lax.broadcasted_iota(jnp.int32, (32, 24, 128), 0)
    inner_row = lax.broadcasted_iota(jnp.int32, (32, 24, 128), 1)
    lane3 = lax.broadcasted_iota(jnp.int32, (32, 24, 128), 2)
    src_of = (
        jnp.where(inner_row >= 6, 1, 0) + jnp.where(inner_row >= 12, 1, 0) + jnp.where(inner_row >= 18, 1, 0)
    )
    want = (inner_row - 6 * src_of + 1).astype(F32).reshape(768, 128)
    src_flat = src_of.reshape(768, 128)

    def pick_matrix(a, p, q):
        dp, qq, cc = group // 8, (group // 2) % 4, group % 2
        pp = (me[p] + dp) % 4
        expert = STRIDE[a] * me[a] + STRIDE[p] * pp + STRIDE[q] * qq + STRIDE[CORE] * cc
        return jnp.where(expert == lane3, 1.0, 0.0).reshape(768, 128).astype(BF)

    sent = None
    built = None
    p1 = []
    for i, (c0, nc, cw, a, p, q) in enumerate(PLAN):
        g = GDIMS.index(a)
        pb = k[f"pb{g}"]
        if i < len(GDIMS):
            for cp in m_cp[g]:
                cp.wait_recv()
        if i < len(GDIMS) or built[g] != (p, q):
            pick = pick_matrix(a, p, q)
            if i == 0:
                for cp in p_cp:
                    cp.wait_recv()
                sent = jnp.zeros((768, 1), F32)
            for s in range(4):
                marks = jnp.dot(pick, k[f"mg{g}"][s], preferred_element_type=F32)
                hit = (marks == want) & (src_flat == s)
                pb[:, s * 128 : (s + 1) * 128] = jnp.where(hit, 1.0, 0.0).astype(BF)
                if i == 0:
                    weights = jnp.dot(pick, k["pg"][s], preferred_element_type=F32)
                    sent = sent + jnp.sum(jnp.where(hit, weights, 0.0), -1, keepdims=True)
            built = dict(built or {})
            built[g] = (p, q)
        for cp in ag[i]:
            cp.wait_recv()
        rows = jnp.dot(pb[...], k[f"tok{i}"][...].reshape(512, cw), preferred_element_type=F32)
        if i == 0:
            lane = lax.broadcasted_iota(jnp.int32, (768, cw), 1)
            rows = jnp.where(lane >= nc, sent, rows)
        rows = rows.reshape(4, 8, 3, 8, cw).astype(BF)
        k[f"sb{i}"][...] = rows[1:]
        k[f"b1_{i}"][me[p]] = rows[0]
        p1.append([
            launch(k[f"sb{i}"].at[d - 1], k[f"b1_{i}"].at[me[p]], k["s_p1"].at[i, d - 1], k["r_p1"].at[i, d - 1], ring_offset(p, d))
            for d in (2, 1, 3)
        ])

    p2 = []
    for i, (c0, nc, cw, a, p, q) in enumerate(PLAN):
        for cp in p1[i]:
            cp.wait_recv()
        others = OTHER[a]
        spot = tuple(slice(None) if o == p else me[o] for o in others)
        b1, fin = k[f"b1_{i}"], k[f"fin{i}"]
        cps = []
        n = 0
        for dq in (2, 1, 3, 0):
            for dc in (0, 1):
                if dq == 0 and dc == 0:
                    continue
                t = [0, 0, 0, 0]
                t[q], t[CORE] = dq, dc
                slot = coord(q, dq) * 2 + coord(CORE, dc)
                cps.append(launch(b1.at[:, slot], fin.at[spot], k["s_p2"].at[i, n], k["r_p2"].at[i, n], tuple(t)))
                n += 1
        p2.append(cps)
        fin[spot] = b1[:, me[q] * 2 + me[CORE]]

    k["normedt"][...] = normed.astype(F32).T.astype(BF)
    w_copy.wait()
    hid_copy.wait()

    weight_col = None
    out_cps = []
    for i, (c0, nc, cw, a, p, q) in enumerate(PLAN):
        for cp in p2[i]:
            cp.wait_recv()
        rows = k[f"fin{i}"][...].reshape(96, 8, cw).astype(F32).reshape(768, cw)
        if i == 0:
            weight_col = rows[:, nc : nc + 1]
            rows = rows[:, :nc]
        rows_b = rows.astype(BF)
        k[f"scs{i}"][...] = (weight_col * rows).astype(BF)
        cp = pltpu.make_async_copy(k[f"scs{i}"], k["sc_h"].at[:, pl.ds(c0, nc)], k["loc"].at[2 + i])
        cp.start()
        out_cps.append(cp)
        for f0, fn in FBLK:
            part = lax.dot_general(
                rows_b, k["w"][f0 : f0 + fn, c0 : c0 + nc], (((1,), (1,)), ((), ())), preferred_element_type=F32
            )
            if i == 0:
                k["acc"][:, f0 : f0 + fn] = part
            else:
                k["acc"][:, f0 : f0 + fn] += part

    slot_score = jnp.zeros((768, 1), F32)
    for f0, fn in FBLK:
        slot_score = slot_score + jnp.sum(
            k["acc"][:, f0 : f0 + fn] * k["hid"][:, f0 : f0 + fn].astype(F32), -1, keepdims=True
        )
    packed = jnp.sum(jnp.where(lane3 == inner_row, slot_score.reshape(32, 24, 1), 0.0), 1)
    k["rsc"][...] = packed.reshape(32, 1, 128)
    mine = me[Z] * 8 + me[X] * 2 + me[CORE]
    for t in spread(plane_offsets((Z, X, CORE))):
        there = coord(Z, t[Z]) * 8 + coord(X, t[X]) * 2 + coord(CORE, t[CORE])
        cp = remote(k["rsc"].at[there], k["rr"].at[mine, me[Y]], k["s_ret"], k["r_ret"], t)
        cp.start()
    k["rr"][mine, me[Y]] = k["rsc"][mine]
    for f0, fn in FBLK:
        k["hgs"][:, f0 : f0 + fn] = (weight_col * k["acc"][:, f0 : f0 + fn]).astype(BF)
    cp = pltpu.make_async_copy(k["hgs"], k["hg_h"], k["loc"].at[2 + NCH])
    cp.start()
    out_cps.append(cp)
    few = k["rsc"].at[pl.ds(0, 31)]
    pltpu.make_async_copy(few, few, k["r_ret"]).wait()
    column = k["rr"].at[:, me[Y]]
    y_cp = [
        launch(column, column, k["s_rety"].at[d - 1], k["r_rety"].at[d - 1], ring_offset(Y, d)) for d in (2, 1, 3)
    ]
    for cp in y_cp:
        cp.wait_recv()

    back = k["rr"][...].reshape(128, 128)
    mt = k["mt"][...]
    prob = k["prob"][...]
    score = jnp.zeros((128, 128), F32)
    for r in range(6):
        one = jnp.sum(jnp.where(t_col == 6 * me[Y] + r, back, 0.0), -1, keepdims=True)
        score = score + jnp.where(mt == float(r + 1), one, 0.0)
    grad_t = prob * (score - jnp.sum(prob * score, 0, keepdims=True))
    grad = grad_t.T
    hi = grad.astype(BF)
    lo = (grad - hi.astype(F32)).astype(BF)
    local = jnp.dot(k["normedt"][...], hi, preferred_element_type=F32) + jnp.dot(
        k["normedt"][...], lo, preferred_element_type=F32
    )
    nt = (((1,), (1,)), ((), ()))
    normed_grad = lax.dot_general(hi, k["rw"][...], nt, preferred_element_type=F32) + lax.dot_general(
        lo, k["rw"][...], nt, preferred_element_type=F32
    )
    floated = k["res"][...].astype(F32)
    inv = lax.rsqrt(jnp.mean(floated * floated, -1, keepdims=True) + 1e-05)
    unit = floated * inv
    gain_local = jnp.sum(normed_grad * unit, 0, keepdims=True)
    k["gv"][...] = jnp.zeros_like(k["gv"])
    for j in range(22):
        k["gv"][j : j + 1, :] = gain_local[:, j * 128 : (j + 1) * 128]
    k["gv"][22:23, 0:64] = gain_local[:, 2816:2880]
    xs = k["xs"]
    xs[pl.ds(0, 360)] = local.reshape(360, 8, 128).astype(BF)
    xs[pl.ds(360, 3)] = k["gv"][...].reshape(3, 8, 128).astype(BF)
    xs[pl.ds(363, 21)] = jnp.zeros((21, 8, 128), BF)

    a1 = []
    for n, (a, others) in enumerate(COLORS):
        for d in (2, 1, 3):
            piece = xs.at[pl.ds(pl.multiple_of(128 * n + 32 * coord(a, d), 32), 32)]
            a1.append(launch(piece, k["ar1"].at[n, d - 1], k["s_a1"].at[n, d - 1], k["r_a1"].at[n, d - 1], ring_offset(a, d)))
    upper = normed_grad * k["gain"][...]
    k["rg"][...] = (inv * (upper - unit * jnp.mean(upper * unit, -1, keepdims=True))).astype(BF)

    for n, (a, others) in enumerate(COLORS):
        for cp in a1[3 * n : 3 * n + 3]:
            cp.wait_recv()
        total = xs[pl.ds(pl.multiple_of(128 * n + 32 * me[a], 32), 32)].astype(F32)
        for d in range(3):
            total = total + k["ar1"][n, d].astype(F32)
        k["as2"][n] = total.astype(BF)
        ring = (SZ[others[1]] * SZ[others[2]], SZ[others[2]], 1)

        def rank(t):
            return sum(coord(o, t[o]) * s for o, s in zip(others, ring))

        here = rank((0, 0, 0, 0))
        for t in spread(plane_offsets(others)):
            cp = remote(k["as2"].at[n, rank(t)], k["ar2"].at[n, here], k["s_a2"].at[n], k["r_a2"].at[n], t)
            cp.start()
        k["ar2"][n, here] = k["as2"][n, here]
    tot = k["tot"]
    for n, (a, others) in enumerate(COLORS):
        few = k["as2"].at[n, pl.ds(0, 31)]
        pltpu.make_async_copy(few, few, k["r_a2"].at[n]).wait()
        ring = (SZ[others[1]] * SZ[others[2]], SZ[others[2]], 1)
        here = sum(me[o] * s for o, s in zip(others, ring))
        done = jnp.sum(k["ar2"][n].astype(F32), 0)
        at = 128 * n + 32 * me[a] + here
        tot[at] = done.astype(BF)
        for t in spread(plane_offsets(others)):
            cp = remote(tot.at[at], tot.at[at], k["s_g2"].at[n], k["r_g2"].at[n], t)
            cp.start()
    g1 = []
    for n, (a, others) in enumerate(COLORS):
        few = k["as2"].at[n, pl.ds(0, 31)]
        pltpu.make_async_copy(few, few, k["r_g2"].at[n]).wait()
        piece = tot.at[pl.ds(pl.multiple_of(128 * n + 32 * me[a], 32), 32)]
        for d in (2, 1, 3):
            g1.append(launch(piece, piece, k["s_g1"].at[n, d - 1], k["r_g1"].at[n, d - 1], ring_offset(a, d)))
    for cp in g1:
        cp.wait_recv()
    for cp in pending:
        cp.wait_send()
    few = k["rsc"].at[pl.ds(0, 31)]
    pltpu.make_async_copy(few, few, k["s_ret"]).wait()
    for n in range(3):
        few = k["as2"].at[n, pl.ds(0, 31)]
        pltpu.make_async_copy(few, few, k["s_a2"].at[n]).wait()
        pltpu.make_async_copy(few, few, k["s_g2"].at[n]).wait()
    for cp in out_cps:
        cp.wait()


def on_device(residual, norm_gain, router_weight, out_grad, expert_ids, hidden, down_weight):
    vm = pl.BlockSpec(memory_space=pltpu.VMEM)
    hbm = pl.BlockSpec(memory_space=pl.ANY)
    dma = pltpu.SemaphoreType.DMA
    scratch = [
        pltpu.VMEM((768, FF), BF), pltpu.VMEM((FF, D), BF), pltpu.VMEM((768, FF), F32), pltpu.VMEM((768, FF), BF),
        pltpu.VMEM((128, 128), F32), pltpu.VMEM((128, 128), F32), pltpu.VMEM((128, 128), BF),
        pltpu.VMEM((128, D), BF), pltpu.VMEM((D, 128), BF), pltpu.VMEM((8, 128), F32),
        pltpu.VMEM((32, 1, 128), F32), pltpu.VMEM((32, 4, 1, 128), F32),
        pltpu.VMEM((384, 8, 128), BF), pltpu.VMEM((3, 3, 32, 8, 128), BF), pltpu.VMEM((3, 32, 8, 128), BF),
        pltpu.VMEM((3, 32, 8, 128), BF), pltpu.VMEM((24, 128), F32), pltpu.VMEM((128, 384), BF),
    ]
    scratch += [pltpu.VMEM((4, 128, 128), BF) for _ in GDIMS]
    scratch += [pltpu.VMEM((4, 128, 128), BF)]
    scratch += [pltpu.VMEM((768, 512), BF) for _ in GDIMS]
    for c0, nc, cw, a, p, q in PLAN:
        sizes = tuple(SZ[o] for o in OTHER[a])
        scratch += [
            pltpu.VMEM((4, 128, cw), BF), pltpu.VMEM((3, 8, 3, 8, cw), BF), pltpu.VMEM((4, 8, 3, 8, cw), BF),
            pltpu.VMEM(sizes + (3, 8, cw), BF), pltpu.VMEM((768, nc), BF),
        ]
    ng = len(GDIMS)
    scratch += [dma((ng, 3)), dma((ng, 3)), dma((3,)), dma((3,)), dma((NCH, 3)), dma((NCH, 3))]
    scratch += [dma((NCH, 3)), dma((NCH, 3)), dma((NCH, 7)), dma((NCH, 7))]
    scratch += [dma(()), dma(()), dma((3,)), dma((3,)), dma((3, 3)), dma((3, 3)), dma((3,)), dma((3,))]
    scratch += [dma((3,)), dma((3,)), dma((3, 3)), dma((3, 3)), dma((3 + NCH,))]
    hidden_grad, scaled, residual_grad, total = pl.pallas_call(
        kernel,
        name="routed",
        out_shape=(
            jax.ShapeDtypeStruct((768, FF), BF),
            jax.ShapeDtypeStruct((768, D), BF),
            jax.ShapeDtypeStruct((128, D), BF),
            jax.ShapeDtypeStruct((384, 8, 128), BF),
        ),
        in_specs=[vm, vm, vm, vm, vm, hbm, hbm],
        out_specs=(hbm, hbm, vm, vm),
        scratch_shapes=scratch,
        compiler_params=pltpu.CompilerParams(
            collective_id=0, has_side_effects=True, vmem_limit_bytes=67043328
        ),
    )(out_grad, residual, norm_gain[None], router_weight, expert_ids.T, hidden[0], down_weight[0])
    weight_grad = lax.dot_general(
        hidden[0], scaled, (((0,), (0,)), ((), ())), preferred_element_type=F32
    )
    router_grad = total[:360].reshape(D, 128).astype(F32)
    gain_grad = total[360:363].reshape(3072)[:D].astype(F32)
    return hidden_grad[None], weight_grad.astype(BF)[None], residual_grad, router_grad, gain_grad


def solution(mesh):
    finer = Mesh(mesh.devices.reshape(4, 4, 2, mesh.shape["dp"]), AX)
    rows = P(AX, None)
    cube = P(AX, None, None)
    return jax.shard_map(
        on_device,
        mesh=finer,
        in_specs=(rows, P(), P(), rows, rows, cube, cube),
        out_specs=(cube, cube, rows, P(), P()),
        check_vma=False,
    )
```

time: 273 us -> 166 us (0.61)
  Pallas kernels: 0 us -> 136 us
  blocking collectives: 84.1 us -> 0 us
  waiting for transfers between devices: 48.6 us -> 0 us
  local copies, waits for them, and re-layouts: 55.6 us -> 13.9 us
  starting transfers between devices: 38 us -> 0 us
  matrix products: 29.3 us -> 11.6 us
  other arithmetic: 14.9 us -> 2.92 us
    pallas_call x0 -> x1, Pallas kernels: none -> 136 us  [on_device(): pl.pallas_call(kernel, name='routed', out_shape=(jax.ShapeDtypeStruct((76...]
    all_to_all x1 -> x0, blocking collectives: 84.1 us -> none  [side_by_side(): lax.all_to_all(both, axis, split_axis=split_dim, concat_axis=concat_dim,...]
    all_to_all x9 -> x0, waiting for transfers between devices: 48.6 us -> none  [the longest x4 18.2 us: sent_to_all(): lax.all_to_all(jnp.broadcast_to(shard[None], (size, *shard.shape)), axis,...]
    all_to_all x9 -> x0, starting transfers between devices: 38 us -> none  [the longest x4 18.4 us: sent_to_all(): lax.all_to_all(jnp.broadcast_to(shard[None], (size, *shard.shape)), axis,...]
    dot_general x5 -> x1, matrix products: 29.3 us -> 11.6 us  [on_device(): lax.dot_general(hidden[0], scaled, (((0,), (0,)), ((), ())), preferred_el...]
    scatter x2 -> x0, local copies, waits for them, and re-layouts: 12.7 us -> none  [the longest x1 8.71 us: on_device(): jnp.zeros((experts * capacity, width), jnp.bfloat16).at[place].set(repeated)]
    all_to_all x3 -> x0, local copies, waits for them, and re-layouts: 9.31 us -> none  [the longest x1 8.18 us: side_by_side(): lax.all_to_all(both, axis, split_axis=split_dim, concat_axis=concat_dim,...]
    unnamed x23 -> x13, local copies, waits for them, and re-layouts: 4.71 us -> 12.6 us
  transfers between devices with their start and end apart: 9 -> 0, of which waited for: 7 -> 0; matrix products, arithmetic and copies ran while one was open for 10% -> 0% of each run, Pallas kernels for 0% -> 0%
where the time goes in v1:
time: 166 us
  Pallas kernels  136 us (82%)
  local copies, waits for them, and re-layouts  13.9 us (8%)
  matrix products  11.6 us (7%)
  other arithmetic  2.92 us (2%)
    pallas_call x1, Pallas kernels, on_device(): pl.pallas_call(kernel, name='routed', out_shape=(jax.ShapeDtypeStruct((76...  136 us
    unnamed x13, local copies, waits for them, and re-layouts  12.6 us
    dot_general x1, matrix products, on_device(): lax.dot_general(hidden[0], scaled, (((0,), (0,)), ((), ())), preferred_el...  11.6 us

profile of v1, /device:TPU:1, one launch (start us, length us, event | category | flops | bytes accessed | tf_op | source)
XLA Modules:
  0.0 165.5 jit_solution(2433635812225407002)
XLA Ops:
  0.6 0.0 copy-start.3
  0.6 0.0 copy-start
  0.7 2.4 %copy.13.refs_0_ = bf16[128,2880]{1,0:T(8,128)(2,1)} copy(bf16[128,2880]{0,1:T(8,128)(2,1)} %param.10) | data formatting | bytes 1474560 | tf_op args[3]
  3.1 2.3 %copy.14.refs_1_ = bf16[128,2880]{1,0:T(8,128)(2,1)} copy(bf16[128,2880]{0,1:T(8,128)(2,1)} %param.7) | data formatting | bytes 1474560 | tf_op args[0]
  5.3 0.0 copy-done.3
  5.3 0.6 broadcast_in_dim.9.refs_2_
  5.9 0.0 copy-done
  5.9 2.4 %copy.12 = bf16[1,768,1440]{2,1,0:T(8,128)(2,1)} copy(bf16[1,768,1440]{1,2,0:T(8,128)(2,1)S(1)} %copy-done) | data formatting | bytes 4423680 | tf_op args[5]
  8.4 136.4 %routed.1 = (bf16[768,1440]{1,0:T(8,128)(2,1)}, bf16[768,2880]{1,0:T(8,128)(2,1)}, bf16[128,2880]{1,0:T(8,128)(2,1)}, bf16[384,8,128]{2,1,0:T(8,128)(2,1)}) custom-call(bf16[128,2880]{1,0:T(8,128)(2,1)} %copy.13.refs_0_, bf16[128,2880]{1,0:T(8,128)(2,1)} %copy.14.refs_1_, f32[1,2880]{1,0:T(1,128)} %broadcast_in_dim.9.refs_2_, bf16[2880,128]{1,0:T(8,128)(2,1)} %refs_3_.1, ...), custom_call_target="tpu_custom_call" | custom-call | tf_op jit(solution)/shard_map/routed/pallas_call | solution.py:430
  144.8 0.0 copy-start.1
  144.8 4.4 %copy.15 = bf16[1,768,1440]{1,2,0:T(8,128)(2,1)} copy(bf16[1,768,1440]{2,1,0:T(8,128)(2,1)} %bitcast.19) | data formatting | bytes 4423680
  149.1 0.0 copy-done.1
  149.1 0.0 copy-start.2
  149.1 11.6 %fusion = bf16[1,1440,2880]{2,1,0:T(8,128)(2,1)} fusion(bf16[768,2880]{1,0:T(8,128)(2,1)} %get-tuple-element.10, bf16[1,768,1440]{1,2,0:T(8,128)(2,1)S(1)} %copy-done.1), kind=kOutput, calls=%fused_computation.1 | convolution fusion | flops 6374246400 | bytes 14929920 | tf_op jit(solution)/shard_map/dot_general | solution.py:446
  160.8 0.0 copy-done.2
  160.8 1.1 copy.16
  161.9 2.3 %bitcast_convert_fusion = f32[2880,128]{1,0:T(8,128)} fusion(bf16[384,8,128]{2,1,0:T(8,128)(2,1)} %get-tuple-element.12), kind=kLoop, calls=%fused_computation.3 | loop fusion | flops 368640 | bytes 2211840 | tf_op jit(solution)/shard_map/convert_element_type | solution.py:449
  164.2 0.7 slice_bitcast_fusion
  164.9 0.6 slice_convert_fusion
Async XLA Ops:
  0.6 4.7 %copy-start.3 = (f32[2880]{0:T(1024)S(1)}, f32[2880]{0:T(1024)}, u32[]{:S(2)}) copy-start(f32[2880]{0:T(1024)} %param.8) | copy-start | bytes 34564
  0.6 5.3 %copy-start = (bf16[1,768,1440]{1,2,0:T(8,128)(2,1)S(1)}, bf16[1,768,1440]{1,2,0:T(8,128)(2,1)}, u32[]{:S(2)}) copy-start(bf16[1,768,1440]{1,2,0:T(8,128)(2,1)} %param.12) | copy-start | bytes 6635524
  144.8 4.4 %copy-start.1 = (bf16[1,768,1440]{1,2,0:T(8,128)(2,1)S(1)}, bf16[1,768,1440]{1,2,0:T(8,128)(2,1)}, u32[]{:S(2)}) copy-start(bf16[1,768,1440]{1,2,0:T(8,128)(2,1)} %param.12) | copy-start | bytes 6635524
  149.1 11.6 %copy-start.2 = (bf16[128,2880]{1,0:T(8,128)(2,1)S(1)}, bf16[128,2880]{1,0:T(8,128)(2,1)}, u32[]{:S(2)}) copy-start(bf16[128,2880]{1,0:T(8,128)(2,1)} %get-tuple-element.15) | copy-start | bytes 2211844

commit v2 on v1

v2 whole, which is shorter than its diff:
```python
import functools

import jax
import jax.numpy as jnp
from jax import lax
from jax.experimental import pallas as pl
from jax.experimental.pallas import tpu as pltpu
from jax.sharding import Mesh
from jax.sharding import PartitionSpec as P

AX = ("ep_0", "ep_1", "ep_2", "dp")
SZ = (4, 4, 2, 4)
Z, X, CORE, Y = 0, 1, 2, 3
STRIDE = (32, 8, 4, 1)
MESH = pl.DeviceIdType.MESH
D = 2880
FF = 1440
BF = jnp.bfloat16
F32 = jnp.float32

PLAN = (
    (0, 640, 640, Y, Z, X),
    (640, 640, 640, Z, X, Y),
    (1280, 640, 640, X, Y, Z),
    (1920, 384, 384, Y, X, Z),
    (2304, 384, 384, Z, Y, X),
    (2688, 192, 256, X, Z, Y),
)
NCH = len(PLAN)
LAST = NCH - 1
HALF = (0, 1920, 2880)
REUSE = {3: 0, 4: 1}
GDIMS = tuple(dict.fromkeys(c[3] for c in PLAN))
FB = 480
NT = (((1,), (1,)), ((), ()))
TN = (((0,), (0,)), ((), ()))
COLORS = ((Z, (X, CORE, Y)), (X, (Z, CORE, Y)), (Y, (Z, X, CORE)))
OTHER = {Z: (X, CORE, Y), X: (Z, CORE, Y), Y: (Z, X, CORE)}


def off(**kw):
    return kw


def plane_offsets(dims):
    out = []
    for a in range(SZ[dims[0]]):
        for b in range(SZ[dims[1]]):
            for c in range(SZ[dims[2]]):
                if (a, b, c) != (0, 0, 0):
                    t = [0, 0, 0, 0]
                    t[dims[0]], t[dims[1]], t[dims[2]] = a, b, c
                    out.append(tuple(t))
    return out


def spread(offsets):
    def hops(t):
        return sum(min(t[i], SZ[i] - t[i]) for i in (Z, X, Y))

    return sorted(offsets, key=lambda t: -hops(t))


def ring_offset(dim, d):
    t = [0, 0, 0, 0]
    t[dim] = d
    return tuple(t)


def all_peers():
    peers = []
    for c in PLAN:
        for d in (1, 2, 3):
            peers += [ring_offset(c[3], d), ring_offset(c[4], d)]
        for dq in range(4):
            for dc in range(2):
                if dq or dc:
                    t = [0, 0, 0, 0]
                    t[c[5]], t[CORE] = dq, dc
                    peers.append(tuple(t))
    peers += plane_offsets((Z, X, CORE))
    peers += [ring_offset(Y, d) for d in (1, 2, 3)]
    for a, others in COLORS:
        peers += [ring_offset(a, d) for d in (1, 2, 3)]
        peers += plane_offsets(others)
    return list(dict.fromkeys(peers))


PEERS = all_peers()


def inverse_of(t):
    return tuple((SZ[i] - t[i]) % SZ[i] for i in range(4))


def kernel(*refs):
    names = (
        ["og", "res", "gain", "rw", "ids", "hid_h", "w_h"]
        + ["hg_h", "wg_h", "rg", "tot"]
        + ["hid", "w", "acc", "hgs", "mt", "prob", "normedt", "gc"]
        + ["rsc", "rr", "xs", "ar1", "as2", "ar2", "gv", "rows"]
    )
    ng = len(GDIMS)
    names += [f"mg{g}" for g in range(ng)] + ["pg"] + [f"pb{g}" for g in range(ng)]
    names += [f"pick{g}" for g in range(ng)]
    names += [f"perm{a}" for a in (Z, X)]
    for i in range(NCH):
        names += [f"tok{i}", f"sel{i}", f"b1_{i}", f"fin{i}"] + ([f"wgs{i}"] if i not in REUSE else [])
    names += ["s_m", "r_m", "s_p", "r_p", "s_ag", "r_ag", "s_p1", "r_p1", "s_p2", "r_p2"]
    names += ["s_ret", "r_ret", "s_rety", "r_rety", "s_a1", "r_a1", "s_a2", "r_a2"]
    names += ["s_g2", "r_g2", "s_g1", "r_g1", "loc"]
    assert len(names) == len(refs)
    k = dict(zip(names, refs))
    me = [lax.axis_index(a) for a in AX]

    def dev(t):
        return tuple(
            lax.rem(me[i] + t[i], SZ[i]) if t[i] else me[i] for i in range(4)
        )

    def coord(dim, d):
        return lax.rem(me[dim] + d, SZ[dim]) if d else me[dim]

    def remote(src, dst, ssem, rsem, t):
        return pltpu.make_async_remote_copy(
            src_ref=src, dst_ref=dst, send_sem=ssem, recv_sem=rsem,
            device_id=dev(t), device_id_type=MESH,
        )

    pending = []

    def launch(src, dst, ssem, rsem, t):
        cp = remote(src, dst, ssem, rsem, t)
        cp.start()
        pending.append(cp)
        return cp

    barrier = pltpu.get_barrier_semaphore()
    for t in PEERS:
        pl.semaphore_signal(barrier, inc=1, device_id=dev(t), device_id_type=MESH)
    w_copy = pltpu.make_async_copy(k["w_h"], k["w"], k["loc"].at[0])
    w_copy.start()
    hid_copy = pltpu.make_async_copy(k["hid_h"], k["hid"], k["loc"].at[1])
    hid_copy.start()

    e_row = lax.broadcasted_iota(jnp.int32, (128, 128), 0)
    t_col = lax.broadcasted_iota(jnp.int32, (128, 128), 1)
    match = e_row == k["ids"][0:1, :]
    for j in range(1, 4):
        match = match | (e_row == k["ids"][j : j + 1, :])
    matchf = match.astype(F32)
    earlier = jnp.where(e_row < t_col, 1.0, 0.0).astype(BF)
    count = jnp.dot(matchf.astype(BF), earlier, preferred_element_type=F32)
    mt = matchf * (count + 1.0)
    k["mt"][...] = mt
    for g, a in enumerate(GDIMS):
        k[f"mg{g}"][me[a]] = mt.astype(BF)
    nl, cl = PLAN[LAST][1:3]
    k[f"tok{LAST}"][nl:cl, :] = jnp.zeros((cl - nl, 512), BF)

    group = lax.broadcasted_iota(jnp.int32, (32, 24, 128), 0)
    inner_row = lax.broadcasted_iota(jnp.int32, (32, 24, 128), 1)
    lane3 = lax.broadcasted_iota(jnp.int32, (32, 24, 128), 2)
    src_of = (
        jnp.where(inner_row >= 6, 1, 0) + jnp.where(inner_row >= 12, 1, 0) + jnp.where(inner_row >= 18, 1, 0)
    )
    want = (inner_row - 6 * src_of + 1).astype(F32).reshape(768, 128)
    src_flat = src_of.reshape(768, 128)
    for g, a in enumerate(GDIMS):
        o = OTHER[a]
        n1, n2 = SZ[o[1]] * SZ[o[2]], SZ[o[2]]
        expert = STRIDE[a] * me[a] + STRIDE[o[0]] * (group // n1)
        expert = expert + STRIDE[o[1]] * ((group // n2) % SZ[o[1]]) + STRIDE[o[2]] * (group % n2)
        k[f"pick{g}"][...] = jnp.where(expert == lane3, 1.0, 0.0).reshape(768, 128).astype(BF)
    eye = e_row == t_col
    for j in range(23):
        n = min(128, D - 128 * j)
        row = k["gain"][pl.ds(128 * j, n)].reshape(1, n)
        col = jnp.sum(jnp.where(eye[:n, :n], row, 0.0), -1, keepdims=True)
        k["gc"][128 * j : 128 * j + n, :] = jnp.broadcast_to(col, (n, 128))
    pl.semaphore_wait(barrier, len(PEERS))

    m_cp = []
    for g, a in enumerate(GDIMS):
        own = k[f"mg{g}"].at[me[a]]
        m_cp.append([
            launch(own, own, k["s_m"].at[g, d - 1], k["r_m"].at[g, d - 1], ring_offset(a, d))
            for d in (2, 1, 3)
        ])
    ag = [[] for _ in PLAN]

    def gather(i, ds):
        c0, nc, cw, a, p, q = PLAN[i]
        src = k["og"].at[pl.ds(c0, nc)]
        dst = k[f"tok{i}"].at[pl.ds(0, nc), pl.ds(pl.multiple_of(me[a] * 128, 128), 128)]
        for d in ds:
            ag[i].append(
                launch(src, dst, k["s_ag"].at[i, d - 1], k["r_ag"].at[i, d - 1], ring_offset(a, d))
            )

    for i in (0, 1, 2):
        gather(i, (2, 1, 3))
    for i in (3, 4, 5):
        gather(i, (1, 3))
    for i, (c0, nc, cw, a, p, q) in enumerate(PLAN):
        k[f"tok{i}"][0:nc, pl.ds(pl.multiple_of(me[a] * 128, 128), 128)] = k["og"][c0 : c0 + nc, :]

    floated = k["res"][...].astype(F32)
    inv = lax.rsqrt(jnp.mean(floated * floated, 0, keepdims=True) + 1e-05)
    normed = (floated * inv * k["gc"][...]).astype(BF)
    k["normedt"][...] = normed
    logits = lax.dot_general(k["rw"][...], normed, TN, preferred_element_type=F32)
    expo = jnp.where(match, jnp.exp(logits), 0.0)
    prob = expo / jnp.sum(expo, 0, keepdims=True)
    k["prob"][...] = prob
    pa = PLAN[LAST][3]
    k["pg"][me[pa]] = prob.astype(BF)
    own = k["pg"].at[me[pa]]
    p_cp = [
        launch(own, own, k["s_p"].at[d - 1], k["r_p"].at[d - 1], ring_offset(pa, d)) for d in (2, 1, 3)
    ]

    p1 = {}

    def first_ring(i):
        c0, nc, cw, a, p, q = PLAN[i]
        g = GDIMS.index(a)
        pb = k[f"pb{g}"]
        if i < len(GDIMS):
            for cp in m_cp[g]:
                cp.wait_recv()
            for s in range(4):
                marks = jnp.dot(k[f"pick{g}"][...], k[f"mg{g}"][s], preferred_element_type=F32)
                hit = (marks == want) & (src_flat == s)
                pb[:, s * 128 : (s + 1) * 128] = jnp.where(hit, 1.0, 0.0).astype(BF)
        for cp in ag[i]:
            cp.wait_recv()
        rows = lax.dot_general(pb[...], k[f"tok{i}"][...], NT, preferred_element_type=F32)
        if i == LAST:
            for cp in p_cp:
                cp.wait_recv()
            sent = jnp.zeros((768, 128), F32)
            for s in range(4):
                weights = jnp.dot(k[f"pick{g}"][...], k["pg"][s], preferred_element_type=F32)
                sent = sent + pb[:, s * 128 : (s + 1) * 128].astype(F32) * weights
            sent = jnp.sum(sent, -1, keepdims=True)
            lane = lax.broadcasted_iota(jnp.int32, (768, cw), 1)
            rows = jnp.where(lane >= nc, sent, rows)
        others = OTHER[a]
        sel, b1 = k[f"sel{i}"], k[f"b1_{i}"]
        sel[...] = rows.reshape(tuple(SZ[o] for o in others) + (3, 8, cw)).astype(BF)
        cps = []
        for d in (2, 1, 3):
            spot = tuple(coord(p, d) if o == p else slice(None) for o in others)
            cps.append(launch(sel.at[spot], b1.at[me[p]], k["s_p1"].at[i, d - 1], k["r_p1"].at[i, d - 1], ring_offset(p, d)))
        p1[i] = cps
        b1[me[p]] = sel[tuple(me[p] if o == p else slice(None) for o in others)]

    for i in (0, 1, 2):
        first_ring(i)
    for i in (3, 4, 5):
        gather(i, (2,))

    slot = lax.broadcasted_iota(jnp.int32, (768, 128), 0)
    lane = lax.broadcasted_iota(jnp.int32, (768, 128), 1)
    src = (slot * 10923) // 65536
    rest = slot - 6 * src
    from_z = (src % 32) * 24 + (src // 32) * 6 + rest
    from_x = ((src // 32) * 8 + src % 8) * 24 + ((src // 8) % 4) * 6 + rest
    for a, origin in ((Z, from_z), (X, from_x)):
        for j in range(6):
            k[f"perm{a}"][:, 128 * j : 128 * j + 128] = jnp.where(origin == lane + 128 * j, 1.0, 0.0).astype(BF)
    w_copy.wait()
    hid_copy.wait()

    p2 = {}

    def second_ring(i):
        c0, nc, cw, a, p, q = PLAN[i]
        for cp in p1[i]:
            cp.wait_recv()
        others = OTHER[a]
        left = tuple(o for o in others if o != p)
        spot = tuple(slice(None) if o == p else me[o] for o in others)
        b1, fin = k[f"b1_{i}"], k[f"fin{i}"]

        def part_of(dq, dc):
            return (slice(None),) + tuple(coord(q, dq) if o == q else coord(CORE, dc) for o in left)

        cps = []
        n = 0
        for dq in (2, 1, 3, 0):
            for dc in (0, 1):
                if dq == 0 and dc == 0:
                    continue
                t = [0, 0, 0, 0]
                t[q], t[CORE] = dq, dc
                cps.append(launch(b1.at[part_of(dq, dc)], fin.at[spot], k["s_p2"].at[i, n], k["r_p2"].at[i, n], tuple(t)))
                n += 1
        p2[i] = cps
        fin[spot] = b1[part_of(0, 0)]

    def arrived(i):
        c0, nc, cw, a, p, q = PLAN[i]
        for cp in p2[i]:
            cp.wait_recv()
        rows = k[f"fin{i}"][...].reshape(96, 8, cw).astype(F32).reshape(768, cw)
        if a != Y:
            rows = jnp.dot(k[f"perm{a}"][...], rows.astype(BF), preferred_element_type=F32)
        weight = None
        if i == LAST:
            spot = lax.broadcasted_iota(jnp.int32, (16, cw), 1)
            weight = rows[:, nc : nc + 1], lax.dot_general(
                jnp.where(spot == nc, 1.0, 0.0).astype(BF), rows.astype(BF), NT, preferred_element_type=F32
            )[0:1]
            rows = rows[:, :nc]
        k["rows"][:, c0 : c0 + nc] = rows.astype(BF)
        return weight

    def inner_part(h):
        cols = slice(HALF[h], HALF[h + 1])

        def step(n, carry):
            at = pl.ds(pl.multiple_of(n * FB, FB), FB)
            part = lax.dot_general(k["w"][at, cols], k["rows"][:, cols], NT, preferred_element_type=F32)
            if h == 0:
                k["acc"][at, :] = part
            else:
                k["acc"][at, :] += part
            return carry

        lax.fori_loop(0, FF // FB, step, 0)

    for i in (0, 1, 2):
        second_ring(i)
    for i in (3, 4, 5):
        first_ring(i)
    for i in (0, 1, 2):
        arrived(i)
    for i in (3, 4, 5):
        second_ring(i)
    inner_part(0)
    for i in (3, 4, 5):
        weight = arrived(i)
    weight_col, weight_row = weight
    inner_part(1)

    out_cps = {}

    def weight_grad(i):
        c0, nc = PLAN[i][:2]
        scaled = (weight_col * k["rows"][:, c0 : c0 + nc].astype(F32)).astype(BF)
        out = k[f"wgs{REUSE.get(i, i)}"]
        if i in REUSE:
            out_cps[REUSE[i]].wait()

        def step(n, carry):
            at = pl.ds(pl.multiple_of(n * FB, FB), FB)
            out[at, 0:nc] = jnp.dot(k["hid"][at, :], scaled, preferred_element_type=F32).astype(BF)
            return carry

        lax.fori_loop(0, FF // FB, step, 0)
        src = out.at[:, pl.ds(0, nc)] if i in REUSE else out
        cp = pltpu.make_async_copy(src, k["wg_h"].at[:, pl.ds(c0, nc)], k["loc"].at[2 + i])
        cp.start()
        out_cps[i] = cp

    slot_score = jnp.sum(k["acc"][...] * k["hid"][...].astype(F32), 0, keepdims=True)
    hi = slot_score.astype(BF)
    left = slot_score - hi.astype(F32)
    mid = left.astype(BF)
    lo = (left - mid.astype(F32)).astype(BF)
    g_row = lax.broadcasted_iota(jnp.int32, (32, 768), 0)
    g_lane = lax.broadcasted_iota(jnp.int32, (32, 768), 1)
    inside = (g_lane >= g_row * 24) & (g_lane < g_row * 24 + 24)
    place = jnp.where(inner_row == lane3, 1.0, 0.0).reshape(768, 128).astype(BF)
    packed = jnp.zeros((32, 128), F32)
    for part in (hi, mid, lo):
        spread_out = jnp.where(inside, part.astype(F32), 0.0).astype(BF)
        packed = packed + jnp.dot(spread_out, place, preferred_element_type=F32)
    k["rsc"][...] = packed.reshape(32, 1, 128)
    mine = me[Z] * 8 + me[X] * 2 + me[CORE]
    for t in spread(plane_offsets((Z, X, CORE))):
        there = coord(Z, t[Z]) * 8 + coord(X, t[X]) * 2 + coord(CORE, t[CORE])
        cp = remote(k["rsc"].at[there], k["rr"].at[mine, me[Y]], k["s_ret"], k["r_ret"], t)
        cp.start()
    k["rr"][mine, me[Y]] = k["rsc"][mine]
    k["hgs"][...] = (weight_row * k["acc"][...]).astype(BF)
    cp = pltpu.make_async_copy(k["hgs"], k["hg_h"], k["loc"].at[2 + NCH])
    cp.start()
    out_cps[NCH] = cp
    weight_grad(0)
    few = k["rsc"].at[pl.ds(0, 31)]
    pltpu.make_async_copy(few, few, k["r_ret"]).wait()
    column = k["rr"].at[:, me[Y]]
    y_cp = [
        launch(column, column, k["s_rety"].at[d - 1], k["r_rety"].at[d - 1], ring_offset(Y, d)) for d in (2, 1, 3)
    ]
    weight_grad(1)
    for cp in y_cp:
        cp.wait_recv()

    back = k["rr"][...].reshape(128, 128)
    mt = k["mt"][...]
    prob = k["prob"][...]
    score = jnp.zeros((128, 128), F32)
    for r in range(6):
        one = jnp.sum(jnp.where(t_col == 6 * me[Y] + r, back, 0.0), -1, keepdims=True)
        score = score + jnp.where(mt == float(r + 1), one, 0.0)
    grad_t = prob * (score - jnp.sum(prob * score, 0, keepdims=True))
    grad = grad_t.T

    def halves(v):
        top = v.astype(BF)
        return top, (v - top.astype(F32)).astype(BF)

    hi, lo = halves(grad)
    local = jnp.dot(k["normedt"][...], hi, preferred_element_type=F32) + jnp.dot(
        k["normedt"][...], lo, preferred_element_type=F32
    )
    hi, lo = halves(grad_t)
    normed_grad = jnp.dot(k["rw"][...], hi, preferred_element_type=F32) + jnp.dot(
        k["rw"][...], lo, preferred_element_type=F32
    )
    floated = k["res"][...].astype(F32)
    inv = lax.rsqrt(jnp.mean(floated * floated, 0, keepdims=True) + 1e-05)
    unit = floated * inv
    gain_col = jnp.sum(normed_grad * unit, -1, keepdims=True)
    k["gv"][...] = jnp.zeros_like(k["gv"])
    for j in range(23):
        n = min(128, D - 128 * j)
        col = gain_col[128 * j : 128 * j + n]
        k["gv"][j : j + 1, 0:n] = jnp.sum(jnp.where(eye[:n, :n], col, 0.0), 0, keepdims=True)
    xs = k["xs"]
    xs[pl.ds(0, 360)] = local.reshape(360, 8, 128).astype(BF)
    xs[pl.ds(360, 3)] = k["gv"][...].reshape(3, 8, 128).astype(BF)
    xs[pl.ds(363, 21)] = jnp.zeros((21, 8, 128), BF)

    a1 = []
    for n, (a, others) in enumerate(COLORS):
        for d in (2, 1, 3):
            piece = xs.at[pl.ds(pl.multiple_of(128 * n + 32 * coord(a, d), 32), 32)]
            a1.append(launch(piece, k["ar1"].at[n, d - 1], k["s_a1"].at[n, d - 1], k["r_a1"].at[n, d - 1], ring_offset(a, d)))
    upper = normed_grad * k["gc"][...]
    k["rg"][...] = (inv * (upper - unit * jnp.mean(upper * unit, 0, keepdims=True))).astype(BF)
    weight_grad(2)

    for n, (a, others) in enumerate(COLORS):
        for cp in a1[3 * n : 3 * n + 3]:
            cp.wait_recv()
        total = xs[pl.ds(pl.multiple_of(128 * n + 32 * me[a], 32), 32)].astype(F32)
        for d in range(3):
            total = total + k["ar1"][n, d].astype(F32)
        k["as2"][n] = total.astype(BF)
        ring = (SZ[others[1]] * SZ[others[2]], SZ[others[2]], 1)

        def rank(t):
            return sum(coord(o, t[o]) * s for o, s in zip(others, ring))

        here = rank((0, 0, 0, 0))
        for t in spread(plane_offsets(others)):
            cp = remote(k["as2"].at[n, rank(t)], k["ar2"].at[n, here], k["s_a2"].at[n], k["r_a2"].at[n], t)
            cp.start()
        k["ar2"][n, here] = k["as2"][n, here]
    weight_grad(3)
    tot = k["tot"]
    for n, (a, others) in enumerate(COLORS):
        few = k["as2"].at[n, pl.ds(0, 31)]
        pltpu.make_async_copy(few, few, k["r_a2"].at[n]).wait()
        ring = (SZ[others[1]] * SZ[others[2]], SZ[others[2]], 1)
        here = sum(me[o] * s for o, s in zip(others, ring))
        done = jnp.sum(k["ar2"][n].astype(F32), 0)
        at = 128 * n + 32 * me[a] + here
        tot[at] = done.astype(BF)
        for t in spread(plane_offsets(others)):
            cp = remote(tot.at[at], tot.at[at], k["s_g2"].at[n], k["r_g2"].at[n], t)
            cp.start()
    weight_grad(4)
    g1 = []
    for n, (a, others) in enumerate(COLORS):
        few = k["as2"].at[n, pl.ds(0, 31)]
        pltpu.make_async_copy(few, few, k["r_g2"].at[n]).wait()
        piece = tot.at[pl.ds(pl.multiple_of(128 * n + 32 * me[a], 32), 32)]
        for d in (2, 1, 3):
            g1.append(launch(piece, piece, k["s_g1"].at[n, d - 1], k["r_g1"].at[n, d - 1], ring_offset(a, d)))
    weight_grad(5)
    for cp in g1:
        cp.wait_recv()
    for cp in pending:
        cp.wait_send()
    few = k["rsc"].at[pl.ds(0, 31)]
    pltpu.make_async_copy(few, few, k["s_ret"]).wait()
    for n in range(3):
        few = k["as2"].at[n, pl.ds(0, 31)]
        pltpu.make_async_copy(few, few, k["s_a2"].at[n]).wait()
        pltpu.make_async_copy(few, few, k["s_g2"].at[n]).wait()
    for i, cp in out_cps.items():
        if i not in REUSE.values():
            cp.wait()


def finish(hg, wg, rg, tot, hg_o, wg_o, rg_o, router, gain, hg_v, wg_v, rg_v, tot_v, ro_v, rsem, wsem):
    parts = [(tot, tot_v, None)]
    for src, via, dst, rows in ((wg, wg_v, wg_o, 240), (hg, hg_v, hg_o, 480), (rg, rg_v, rg_o, 1440)):
        for r in range(0, src.shape[0], rows):
            at = pl.ds(r, rows)
            parts.append((src.at[at], via.at[at], dst.at[at]))
    reads = [pltpu.make_async_copy(s, v, rsem.at[n]) for n, (s, v, d) in enumerate(parts)]
    for cp in reads:
        cp.start()
    writes = []
    for n, (s, v, d) in enumerate(parts):
        reads[n].wait()
        if d is None:
            ro_v[...] = tot_v[pl.ds(0, 360)].astype(F32).reshape(D, 128)
            cp = pltpu.make_async_copy(ro_v, router, wsem.at[n])
            cp.start()
            writes.append(cp)
            rows = tot_v[pl.ds(360, 3)].astype(F32).reshape(24, 128)
            for j in range(23):
                m = min(128, D - 128 * j)
                gain[pl.ds(128 * j, m)] = rows[j : j + 1, 0:m].reshape(m)
        else:
            cp = pltpu.make_async_copy(v, d, wsem.at[n])
            cp.start()
            writes.append(cp)
    for cp in writes:
        cp.wait()


def on_device(residual, norm_gain, router_weight, out_grad, expert_ids, hidden, down_weight):
    vm = pl.BlockSpec(memory_space=pltpu.VMEM)
    hbm = pl.BlockSpec(memory_space=pl.ANY)
    dma = pltpu.SemaphoreType.DMA
    scratch = [
        pltpu.VMEM((FF, 768), BF), pltpu.VMEM((FF, D), BF), pltpu.VMEM((FF, 768), F32), pltpu.VMEM((FF, 768), BF),
        pltpu.VMEM((128, 128), F32), pltpu.VMEM((128, 128), F32), pltpu.VMEM((D, 128), BF), pltpu.VMEM((D, 128), F32),
        pltpu.VMEM((32, 1, 128), F32), pltpu.VMEM((32, 4, 1, 128), F32),
        pltpu.VMEM((384, 8, 128), BF), pltpu.VMEM((3, 3, 32, 8, 128), BF), pltpu.VMEM((3, 32, 8, 128), BF),
        pltpu.VMEM((3, 32, 8, 128), BF), pltpu.VMEM((24, 128), F32), pltpu.VMEM((768, D), BF),
    ]
    scratch += [pltpu.VMEM((4, 128, 128), BF) for _ in GDIMS]
    scratch += [pltpu.VMEM((4, 128, 128), BF)]
    scratch += [pltpu.VMEM((768, 512), BF) for _ in GDIMS]
    scratch += [pltpu.VMEM((768, 128), BF) for _ in GDIMS]
    scratch += [pltpu.VMEM((768, 768), BF) for _ in range(2)]
    for i, (c0, nc, cw, a, p, q) in enumerate(PLAN):
        sizes = tuple(SZ[o] for o in OTHER[a])
        scratch += [
            pltpu.VMEM((cw, 512), BF), pltpu.VMEM(sizes + (3, 8, cw), BF),
            pltpu.VMEM((4,) + tuple(SZ[o] for o in OTHER[a] if o != p) + (3, 8, cw), BF),
            pltpu.VMEM(sizes + (3, 8, cw), BF),
        ]
        if i not in REUSE:
            scratch.append(pltpu.VMEM((FF, nc), BF))
    ng = len(GDIMS)
    scratch += [dma((ng, 3)), dma((ng, 3)), dma((3,)), dma((3,)), dma((NCH, 3)), dma((NCH, 3))]
    scratch += [dma((NCH, 3)), dma((NCH, 3)), dma((NCH, 7)), dma((NCH, 7))]
    scratch += [dma(()), dma(()), dma((3,)), dma((3,)), dma((3, 3)), dma((3, 3)), dma((3,)), dma((3,))]
    scratch += [dma((3,)), dma((3,)), dma((3, 3)), dma((3, 3)), dma((3 + NCH,))]
    hidden_grad, weight_grad, residual_grad, total = pl.pallas_call(
        kernel,
        name="routed",
        out_shape=(
            jax.ShapeDtypeStruct((FF, 768), BF),
            jax.ShapeDtypeStruct((FF, D), BF),
            jax.ShapeDtypeStruct((D, 128), BF),
            jax.ShapeDtypeStruct((384, 8, 128), BF),
        ),
        in_specs=[vm, vm, vm, vm, vm, hbm, hbm],
        out_specs=(hbm, hbm, vm, vm),
        scratch_shapes=scratch,
        compiler_params=pltpu.CompilerParams(
            collective_id=0, has_side_effects=True, vmem_limit_bytes=67043328
        ),
    )(out_grad.T, residual.T, norm_gain, router_weight, expert_ids.T, hidden[0].T, down_weight[0])
    nparts = 1 + FF // 240 + FF // 480 + D // 1440
    hidden_grad, weight_grad, residual_grad, router_grad, gain_grad = pl.pallas_call(
        finish,
        name="finish",
        out_shape=(
            jax.ShapeDtypeStruct((FF, 768), BF),
            jax.ShapeDtypeStruct((FF, D), BF),
            jax.ShapeDtypeStruct((D, 128), BF),
            jax.ShapeDtypeStruct((D, 128), F32),
            jax.ShapeDtypeStruct((D,), F32),
        ),
        in_specs=[hbm, hbm, hbm, hbm],
        out_specs=(hbm, hbm, hbm, hbm, vm),
        scratch_shapes=[
            pltpu.VMEM((FF, 768), BF), pltpu.VMEM((FF, D), BF), pltpu.VMEM((D, 128), BF),
            pltpu.VMEM((384, 8, 128), BF), pltpu.VMEM((D, 128), F32), dma((nparts,)), dma((nparts,)),
        ],
        compiler_params=pltpu.CompilerParams(vmem_limit_bytes=67043328),
    )(hidden_grad, weight_grad, residual_grad, total)
    return hidden_grad.T[None], weight_grad[None], residual_grad.T, router_grad, gain_grad


def solution(mesh):
    finer = Mesh(mesh.devices.reshape(4, 4, 2, mesh.shape["dp"]), AX)
    rows = P(AX, None)
    cube = P(AX, None, None)
    return jax.shard_map(
        on_device,
        mesh=finer,
        in_specs=(rows, P(), P(), rows, rows, cube, cube),
        out_specs=(cube, cube, rows, P(), P()),
        check_vma=False,
    )
```

time: 166 us -> 115 us (0.69)
  Pallas kernels: 136 us -> 114 us
  local copies, waits for them, and re-layouts: 13.9 us -> 0 us
  matrix products: 11.6 us -> 0 us
  other arithmetic: 2.92 us -> 0 us
    pallas_call x1 -> x2, Pallas kernels: 136 us -> 114 us  [the longest x1 104 us: on_device(): pl.pallas_call(kernel, name='routed', out_shape=(jax.ShapeDtypeStruct((FF...]
    unnamed x13 -> x0, local copies, waits for them, and re-layouts: 12.6 us -> none
    dot_general x1 -> x0, matrix products: 11.6 us -> none  [on_device(): lax.dot_general(hidden[0], scaled, (((0,), (0,)), ((), ())), preferred_el...]
    convert_element_type x2 -> x0, other arithmetic: 2.92 us -> none  [the longest x1 2.32 us: on_device(): router_grad = total[:360].reshape(D, 128).astype(F32)]
where the time goes in v2:
time: 115 us
  Pallas kernels  114 us (99%)
    pallas_call x1, Pallas kernels, on_device(): pl.pallas_call(kernel, name='routed', out_shape=(jax.ShapeDtypeStruct((FF...  104 us
    pallas_call x1, Pallas kernels, on_device(): pl.pallas_call(finish, name='finish', out_shape=(jax.ShapeDtypeStruct((FF...  10 us

profile of v2, /device:TPU:1, one launch (start us, length us, event | category | flops | bytes accessed | tf_op | source)
XLA Modules:
  0.0 114.8 jit_solution(14934318636417516414)
XLA Ops:
  0.6 103.9 %routed.1 = (bf16[1440,768]{1,0:T(8,128)(2,1)}, bf16[1440,2880]{1,0:T(8,128)(2,1)}, bf16[2880,128]{1,0:T(8,128)(2,1)}, bf16[384,8,128]{2,1,0:T(8,128)(2,1)}) custom-call(bf16[2880,128]{1,0:T(8,128)(2,1)} %bitcast.14, bf16[2880,128]{1,0:T(8,128)(2,1)} %bitcast.15, f32[2880]{0:T(1024)} %refs_2_.1, bf16[2880,128]{1,0:T(8,128)(2,1)} %refs_3_.1, ...), custom_call_target="tpu_custom_call" | custom-call | tf_op jit(solution)/shard_map/routed/pallas_call | solution.py:561
  104.6 10.0 %finish.1 = (bf16[1440,768]{1,0:T(8,128)(2,1)}, bf16[1440,2880]{1,0:T(8,128)(2,1)}, bf16[2880,128]{1,0:T(8,128)(2,1)}, f32[2880,128]{1,0:T(8,128)}, f32[2880]{0:T(1024)}) custom-call(bf16[1440,768]{1,0:T(8,128)(2,1)} %get-tuple-element.14.hg, bf16[1440,2880]{1,0:T(8,128)(2,1)} %get-tuple-element.15.wg, bf16[2880,128]{1,0:T(8,128)(2,1)} %get-tuple-element.16.rg, ...), custom_call_target="tpu_custom_call" | custom-call | tf_op jit(solution)/shard_map/finish/pallas_call | solution.py:578

commit v3 on v2

--- a/solution.py
+++ b/solution.py
@@ -19,27 +19,26 @@
 F32 = jnp.float32
 
 PLAN = (
-    (0, 640, 640, Y, Z, X),
-    (640, 640, 640, Z, X, Y),
-    (1280, 640, 640, X, Y, Z),
-    (1920, 384, 384, Y, X, Z),
-    (2304, 384, 384, Z, Y, X),
-    (2688, 192, 256, X, Z, Y),
+    (0, 384, 384, Y, Z, X),
+    (384, 384, 384, Z, X, Y),
+    (768, 384, 384, X, Y, Z),
+    (1152, 384, 384, Y, X, Z),
+    (1536, 384, 384, Z, Y, X),
+    (1920, 384, 384, X, Z, Y),
+    (2304, 256, 256, Y, Z, X),
+    (2560, 256, 256, Z, X, Y),
+    (2816, 64, 128, X, Y, Z),
 )
 NCH = len(PLAN)
 LAST = NCH - 1
-HALF = (0, 1920, 2880)
-REUSE = {3: 0, 4: 1}
+PARTS = (0, 1152, 2304, 2880)
+OUT_COLS = ((0, 768), (768, 768), (1536, 768), (2304, 576))
 GDIMS = tuple(dict.fromkeys(c[3] for c in PLAN))
 FB = 480
 NT = (((1,), (1,)), ((), ()))
 TN = (((0,), (0,)), ((), ()))
 COLORS = ((Z, (X, CORE, Y)), (X, (Z, CORE, Y)), (Y, (Z, X, CORE)))
 OTHER = {Z: (X, CORE, Y), X: (Z, CORE, Y), Y: (Z, X, CORE)}
-
-
-def off(**kw):
-    return kw
 
 
 def plane_offsets(dims):
@@ -67,30 +66,11 @@
     return tuple(t)
 
 
-def all_peers():
-    peers = []
-    for c in PLAN:
-        for d in (1, 2, 3):
-            peers += [ring_offset(c[3], d), ring_offset(c[4], d)]
-        for dq in range(4):
-            for dc in range(2):
-                if dq or dc:
-                    t = [0, 0, 0, 0]
-                    t[c[5]], t[CORE] = dq, dc
-                    peers.append(tuple(t))
-    peers += plane_offsets((Z, X, CORE))
-    peers += [ring_offset(Y, d) for d in (1, 2, 3)]
-    for a, others in COLORS:
-        peers += [ring_offset(a, d) for d in (1, 2, 3)]
-        peers += plane_offsets(others)
-    return list(dict.fromkeys(peers))
-
-
-PEERS = all_peers()
-
-
-def inverse_of(t):
-    return tuple((SZ[i] - t[i]) % SZ[i] for i in range(4))
+PEERS = [
+    (z, x, c, y)
+    for z in range(4) for x in range(4) for c in range(2) for y in range(4)
+    if (z, x, c, y) != (0, 0, 0, 0)
+]
 
 
 def kernel(*refs):
@@ -98,16 +78,16 @@
         ["og", "res", "gain", "rw", "ids", "hid_h", "w_h"]
         + ["hg_h", "wg_h", "rg", "tot"]
         + ["hid", "w", "acc", "hgs", "mt", "prob", "normedt", "gc"]
-        + ["rsc", "rr", "xs", "ar1", "as2", "ar2", "gv", "rows"]
+        + ["rsc", "rr", "xs", "ar1", "as2", "ar2", "gv", "rows", "wgs0", "wgs1", "wgs3"]
     )
     ng = len(GDIMS)
     names += [f"mg{g}" for g in range(ng)] + ["pg"] + [f"pb{g}" for g in range(ng)]
     names += [f"pick{g}" for g in range(ng)]
     names += [f"perm{a}" for a in (Z, X)]
     for i in range(NCH):
-        names += [f"tok{i}", f"sel{i}", f"b1_{i}", f"fin{i}"] + ([f"wgs{i}"] if i not in REUSE else [])
+        names += [f"tok{i}", f"sel{i}", f"b1_{i}", f"fin{i}"]
     names += ["s_m", "r_m", "s_p", "r_p", "s_ag", "r_ag", "s_p1", "r_p1", "s_p2", "r_p2"]
-    names += ["s_ret", "r_ret", "s_rety", "r_rety", "s_a1", "r_a1", "s_a2", "r_a2"]
+    names += ["s_ret", "r_ret", "s_a1", "r_a1", "s_a2", "r_a2"]
     names += ["s_g2", "r_g2", "s_g1", "r_g1", "loc"]
     assert len(names) == len(refs)
     k = dict(zip(names, refs))
@@ -198,10 +178,8 @@
                 launch(src, dst, k["s_ag"].at[i, d - 1], k["r_ag"].at[i, d - 1], ring_offset(a, d))
             )
 
-    for i in (0, 1, 2):
+    for i in range(NCH):
         gather(i, (2, 1, 3))
-    for i in (3, 4, 5):
-        gather(i, (1, 3))
     for i, (c0, nc, cw, a, p, q) in enumerate(PLAN):
         k[f"tok{i}"][0:nc, pl.ds(pl.multiple_of(me[a] * 128, 128), 128)] = k["og"][c0 : c0 + nc, :]
 
@@ -256,10 +234,8 @@
         p1[i] = cps
         b1[me[p]] = sel[tuple(me[p] if o == p else slice(None) for o in others)]
 
-    for i in (0, 1, 2):
+    for i in range(6):
         first_ring(i)
-    for i in (3, 4, 5):
-        gather(i, (2,))
 
     slot = lax.broadcasted_iota(jnp.int32, (768, 128), 0)
     lane = lax.broadcasted_iota(jnp.int32, (768, 128), 1)
@@ -318,7 +294,7 @@
         return weight
 
     def inner_part(h):
-        cols = slice(HALF[h], HALF[h + 1])
+        cols = slice(PARTS[h], PARTS[h + 1])
 
         def step(n, carry):
             at = pl.ds(pl.multiple_of(n * FB, FB), FB)
@@ -333,35 +309,39 @@
 
     for i in (0, 1, 2):
         second_ring(i)
+    for i in (6, 7, 8):
+        first_ring(i)
     for i in (3, 4, 5):
-        first_ring(i)
+        second_ring(i)
     for i in (0, 1, 2):
         arrived(i)
+    inner_part(0)
+    for i in (6, 7, 8):
+        second_ring(i)
     for i in (3, 4, 5):
-        second_ring(i)
-    inner_part(0)
-    for i in (3, 4, 5):
+        arrived(i)
+    inner_part(1)
+    for i in (6, 7, 8):
         weight = arrived(i)
     weight_col, weight_row = weight
-    inner_part(1)
+    inner_part(2)
 
     out_cps = {}
 
     def weight_grad(i):
-        c0, nc = PLAN[i][:2]
+        c0, nc = OUT_COLS[i]
         scaled = (weight_col * k["rows"][:, c0 : c0 + nc].astype(F32)).astype(BF)
-        out = k[f"wgs{REUSE.get(i, i)}"]
-        if i in REUSE:
-            out_cps[REUSE[i]].wait()
+        out = k[("wgs0", "wgs1", "wgs0", "wgs3")[i]]
+        if i == 2:
+            out_cps[0].wait()
 
         def step(n, carry):
             at = pl.ds(pl.multiple_of(n * FB, FB), FB)
-            out[at, 0:nc] = jnp.dot(k["hid"][at, :], scaled, preferred_element_type=F32).astype(BF)
+            out[at, :] = jnp.dot(k["hid"][at, :], scaled, preferred_element_type=F32).astype(BF)
             return carry
 
         lax.fori_loop(0, FF // FB, step, 0)
-        src = out.at[:, pl.ds(0, nc)] if i in REUSE else out
-        cp = pltpu.make_async_copy(src, k["wg_h"].at[:, pl.ds(c0, nc)], k["loc"].at[2 + i])
+        cp = pltpu.make_async_copy(out, k["wg_h"].at[:, pl.ds(c0, nc)], k["loc"].at[2 + i])
         cp.start()
         out_cps[i] = cp
 
@@ -370,43 +350,34 @@
     left = slot_score - hi.astype(F32)
     mid = left.astype(BF)
     lo = (left - mid.astype(F32)).astype(BF)
-    g_row = lax.broadcasted_iota(jnp.int32, (32, 768), 0)
-    g_lane = lax.broadcasted_iota(jnp.int32, (32, 768), 1)
-    inside = (g_lane >= g_row * 24) & (g_lane < g_row * 24 + 24)
-    place = jnp.where(inner_row == lane3, 1.0, 0.0).reshape(768, 128).astype(BF)
-    packed = jnp.zeros((32, 128), F32)
+    g_row = lax.broadcasted_iota(jnp.int32, (128, 768), 0)
+    g_lane = lax.broadcasted_iota(jnp.int32, (128, 768), 1)
+    inside = (g_lane >= g_row * 6) & (g_lane < g_row * 6 + 6)
+    place = jnp.where(rest == lane, 1.0, 0.0).astype(BF)
+    packed = jnp.zeros((128, 128), F32)
     for part in (hi, mid, lo):
         spread_out = jnp.where(inside, part.astype(F32), 0.0).astype(BF)
         packed = packed + jnp.dot(spread_out, place, preferred_element_type=F32)
-    k["rsc"][...] = packed.reshape(32, 1, 128)
-    mine = me[Z] * 8 + me[X] * 2 + me[CORE]
-    for t in spread(plane_offsets((Z, X, CORE))):
-        there = coord(Z, t[Z]) * 8 + coord(X, t[X]) * 2 + coord(CORE, t[CORE])
-        cp = remote(k["rsc"].at[there], k["rr"].at[mine, me[Y]], k["s_ret"], k["r_ret"], t)
-        cp.start()
-    k["rr"][mine, me[Y]] = k["rsc"][mine]
+    k["rsc"][...] = packed.reshape(128, 1, 128)
+    mine = sum(me[o] * STRIDE[o] for o in range(4))
+    for t in spread(PEERS):
+        there = sum(coord(o, t[o]) * STRIDE[o] for o in range(4))
+        remote(k["rsc"].at[there], k["rr"].at[mine], k["s_ret"], k["r_ret"], t).start()
+    k["rr"][mine] = k["rsc"][mine]
     k["hgs"][...] = (weight_row * k["acc"][...]).astype(BF)
-    cp = pltpu.make_async_copy(k["hgs"], k["hg_h"], k["loc"].at[2 + NCH])
+    cp = pltpu.make_async_copy(k["hgs"], k["hg_h"], k["loc"].at[6])
     cp.start()
-    out_cps[NCH] = cp
+    out_cps[4] = cp
     weight_grad(0)
-    few = k["rsc"].at[pl.ds(0, 31)]
+    few = k["rsc"].at[pl.ds(0, 127)]
     pltpu.make_async_copy(few, few, k["r_ret"]).wait()
-    column = k["rr"].at[:, me[Y]]
-    y_cp = [
-        launch(column, column, k["s_rety"].at[d - 1], k["r_rety"].at[d - 1], ring_offset(Y, d)) for d in (2, 1, 3)
-    ]
-    weight_grad(1)
-    for cp in y_cp:
-        cp.wait_recv()
 
     back = k["rr"][...].reshape(128, 128)
     mt = k["mt"][...]
     prob = k["prob"][...]
     score = jnp.zeros((128, 128), F32)
     for r in range(6):
-        one = jnp.sum(jnp.where(t_col == 6 * me[Y] + r, back, 0.0), -1, keepdims=True)
-        score = score + jnp.where(mt == float(r + 1), one, 0.0)
+        score = score + jnp.where(mt == float(r + 1), back[:, r : r + 1], 0.0)
     grad_t = prob * (score - jnp.sum(prob * score, 0, keepdims=True))
     grad = grad_t.T
 
@@ -443,7 +414,7 @@
             a1.append(launch(piece, k["ar1"].at[n, d - 1], k["s_a1"].at[n, d - 1], k["r_a1"].at[n, d - 1], ring_offset(a, d)))
     upper = normed_grad * k["gc"][...]
     k["rg"][...] = (inv * (upper - unit * jnp.mean(upper * unit, 0, keepdims=True))).astype(BF)
-    weight_grad(2)
+    weight_grad(1)
 
     for n, (a, others) in enumerate(COLORS):
         for cp in a1[3 * n : 3 * n + 3]:
@@ -462,7 +433,7 @@
             cp = remote(k["as2"].at[n, rank(t)], k["ar2"].at[n, here], k["s_a2"].at[n], k["r_a2"].at[n], t)
             cp.start()
         k["ar2"][n, here] = k["as2"][n, here]
-    weight_grad(3)
+    weight_grad(2)
     tot = k["tot"]
     for n, (a, others) in enumerate(COLORS):
         few = k["as2"].at[n, pl.ds(0, 31)]
@@ -475,7 +446,7 @@
         for t in spread(plane_offsets(others)):
             cp = remote(tot.at[at], tot.at[at], k["s_g2"].at[n], k["r_g2"].at[n], t)
             cp.start()
-    weight_grad(4)
+    weight_grad(3)
     g1 = []
     for n, (a, others) in enumerate(COLORS):
         few = k["as2"].at[n, pl.ds(0, 31)]
@@ -483,19 +454,18 @@
         piece = tot.at[pl.ds(pl.multiple_of(128 * n + 32 * me[a], 32), 32)]
         for d in (2, 1, 3):
             g1.append(launch(piece, piece, k["s_g1"].at[n, d - 1], k["r_g1"].at[n, d - 1], ring_offset(a, d)))
-    weight_grad(5)
     for cp in g1:
         cp.wait_recv()
     for cp in pending:
         cp.wait_send()
-    few = k["rsc"].at[pl.ds(0, 31)]
+    few = k["rsc"].at[pl.ds(0, 127)]
     pltpu.make_async_copy(few, few, k["s_ret"]).wait()
     for n in range(3):
         few = k["as2"].at[n, pl.ds(0, 31)]
         pltpu.make_async_copy(few, few, k["s_a2"].at[n]).wait()
         pltpu.make_async_copy(few, few, k["s_g2"].at[n]).wait()
     for i, cp in out_cps.items():
-        if i not in REUSE.values():
+        if i != 0:
             cp.wait()
 
 
@@ -535,9 +505,10 @@
     scratch = [
         pltpu.VMEM((FF, 768), BF), pltpu.VMEM((FF, D), BF), pltpu.VMEM((FF, 768), F32), pltpu.VMEM((FF, 768), BF),
         pltpu.VMEM((128, 128), F32), pltpu.VMEM((128, 128), F32), pltpu.VMEM((D, 128), BF), pltpu.VMEM((D, 128), F32),
-        pltpu.VMEM((32, 1, 128), F32), pltpu.VMEM((32, 4, 1, 128), F32),
+        pltpu.VMEM((128, 1, 128), F32), pltpu.VMEM((128, 1, 128), F32),
         pltpu.VMEM((384, 8, 128), BF), pltpu.VMEM((3, 3, 32, 8, 128), BF), pltpu.VMEM((3, 32, 8, 128), BF),
         pltpu.VMEM((3, 32, 8, 128), BF), pltpu.VMEM((24, 128), F32), pltpu.VMEM((768, D), BF),
+        pltpu.VMEM((FF, 768), BF), pltpu.VMEM((FF, 768), BF), pltpu.VMEM((FF, 576), BF),
     ]
     scratch += [pltpu.VMEM((4, 128, 128), BF) for _ in GDIMS]
     scratch += [pltpu.VMEM((4, 128, 128), BF)]
@@ -551,13 +522,11 @@
             pltpu.VMEM((4,) + tuple(SZ[o] for o in OTHER[a] if o != p) + (3, 8, cw), BF),
             pltpu.VMEM(sizes + (3, 8, cw), BF),
         ]
-        if i not in REUSE:
-            scratch.append(pltpu.VMEM((FF, nc), BF))
     ng = len(GDIMS)
     scratch += [dma((ng, 3)), dma((ng, 3)), dma((3,)), dma((3,)), dma((NCH, 3)), dma((NCH, 3))]
     scratch += [dma((NCH, 3)), dma((NCH, 3)), dma((NCH, 7)), dma((NCH, 7))]
-    scratch += [dma(()), dma(()), dma((3,)), dma((3,)), dma((3, 3)), dma((3, 3)), dma((3,)), dma((3,))]
-    scratch += [dma((3,)), dma((3,)), dma((3, 3)), dma((3, 3)), dma((3 + NCH,))]
+    scratch += [dma(()), dma(()), dma((3, 3)), dma((3, 3)), dma((3,)), dma((3,))]
+    scratch += [dma((3,)), dma((3,)), dma((3, 3)), dma((3, 3)), dma((7,))]
     hidden_grad, weight_grad, residual_grad, total = pl.pallas_call(
         kernel,
         name="routed",

time: 115 us -> 110 us (0.957)
  Pallas kernels: 114 us -> 109 us
    pallas_call x1, Pallas kernels: 104 us -> 99.5 us  [on_device(): pl.pallas_call(kernel, name='routed', out_shape=(jax.ShapeDtypeStruct((FF...]
where the time goes in v3:
time: 110 us
  Pallas kernels  109 us (99%)
    pallas_call x1, Pallas kernels, on_device(): pl.pallas_call(kernel, name='routed', out_shape=(jax.ShapeDtypeStruct((FF...  99.5 us
    pallas_call x1, Pallas kernels, on_device(): pl.pallas_call(finish, name='finish', out_shape=(jax.ShapeDtypeStruct((FF...  10 us

profile of v3, /device:TPU:1, one launch (start us, length us, event | category | flops | bytes accessed | tf_op | source)
XLA Modules:
  0.0 110.3 jit_solution(7374515279991289410)
XLA Ops:
  0.6 99.5 %routed.1 = (bf16[1440,768]{1,0:T(8,128)(2,1)}, bf16[1440,2880]{1,0:T(8,128)(2,1)}, bf16[2880,128]{1,0:T(8,128)(2,1)}, bf16[384,8,128]{2,1,0:T(8,128)(2,1)}) custom-call(bf16[2880,128]{1,0:T(8,128)(2,1)} %bitcast.14, bf16[2880,128]{1,0:T(8,128)(2,1)} %bitcast.15, f32[2880]{0:T(1024)} %refs_2_.1, bf16[2880,128]{1,0:T(8,128)(2,1)} %refs_3_.1, ...), custom_call_target="tpu_custom_call" | custom-call | tf_op jit(solution)/shard_map/routed/pallas_call | solution.py:530
  100.1 10.0 %finish.1 = (bf16[1440,768]{1,0:T(8,128)(2,1)}, bf16[1440,2880]{1,0:T(8,128)(2,1)}, bf16[2880,128]{1,0:T(8,128)(2,1)}, f32[2880,128]{1,0:T(8,128)}, f32[2880]{0:T(1024)}) custom-call(bf16[1440,768]{1,0:T(8,128)(2,1)} %get-tuple-element.14.hg, bf16[1440,2880]{1,0:T(8,128)(2,1)} %get-tuple-element.15.wg, bf16[2880,128]{1,0:T(8,128)(2,1)} %get-tuple-element.16.rg, ...), custom_call_target="tpu_custom_call" | custom-call | tf_op jit(solution)/shard_map/finish/pallas_call | solution.py:547

commit v4 on v3

--- a/solution.py
+++ b/solution.py
@@ -19,19 +19,19 @@
 F32 = jnp.float32
 
 PLAN = (
-    (0, 384, 384, Y, Z, X),
-    (384, 384, 384, Z, X, Y),
-    (768, 384, 384, X, Y, Z),
-    (1152, 384, 384, Y, X, Z),
-    (1536, 384, 384, Z, Y, X),
-    (1920, 384, 384, X, Z, Y),
+    (0, 512, 512, Y, Z, X),
+    (512, 512, 512, Z, X, Y),
+    (1024, 512, 512, X, Y, Z),
+    (1536, 256, 256, Y, X, Z),
+    (1792, 256, 256, Z, Y, X),
+    (2048, 256, 256, X, Z, Y),
     (2304, 256, 256, Y, Z, X),
     (2560, 256, 256, Z, X, Y),
     (2816, 64, 128, X, Y, Z),
 )
 NCH = len(PLAN)
 LAST = NCH - 1
-PARTS = (0, 1152, 2304, 2880)
+PARTS = (0, 1536, 2304, 2880)
 OUT_COLS = ((0, 768), (768, 768), (1536, 768), (2304, 576))
 GDIMS = tuple(dict.fromkeys(c[3] for c in PLAN))
 FB = 480
@@ -75,9 +75,9 @@
 
 def kernel(*refs):
     names = (
-        ["og", "res", "gain", "rw", "ids", "hid_h", "w_h"]
-        + ["hg_h", "wg_h", "rg", "tot"]
-        + ["hid", "w", "acc", "hgs", "mt", "prob", "normedt", "gc"]
+        ["og_h", "res_h", "gain_h", "rw_h", "ids_h", "hid_h", "w_h"]
+        + ["hg_h", "wg_h", "rg_h", "tot_h"]
+        + ["og", "res", "gain", "rw", "ids", "rg", "tot", "hid", "w", "acc", "hgs", "mt", "prob", "normedt", "gc"]
         + ["rsc", "rr", "xs", "ar1", "as2", "ar2", "gv", "rows", "wgs0", "wgs1", "wgs3"]
     )
     ng = len(GDIMS)
@@ -115,6 +115,10 @@
         pending.append(cp)
         return cp
 
+    fetch = {}
+    for n, name in enumerate(("ids", "gain", "og", "res", "rw")):
+        fetch[name] = pltpu.make_async_copy(k[name + "_h"], k[name], k["loc"].at[7 + n])
+        fetch[name].start()
     barrier = pltpu.get_barrier_semaphore()
     for t in PEERS:
         pl.semaphore_signal(barrier, inc=1, device_id=dev(t), device_id_type=MESH)
@@ -125,6 +129,7 @@
 
     e_row = lax.broadcasted_iota(jnp.int32, (128, 128), 0)
     t_col = lax.broadcasted_iota(jnp.int32, (128, 128), 1)
+    fetch["ids"].wait()
     match = e_row == k["ids"][0:1, :]
     for j in range(1, 4):
         match = match | (e_row == k["ids"][j : j + 1, :])
@@ -153,11 +158,13 @@
         expert = expert + STRIDE[o[1]] * ((group // n2) % SZ[o[1]]) + STRIDE[o[2]] * (group % n2)
         k[f"pick{g}"][...] = jnp.where(expert == lane3, 1.0, 0.0).reshape(768, 128).astype(BF)
     eye = e_row == t_col
+    fetch["gain"].wait()
     for j in range(23):
         n = min(128, D - 128 * j)
         row = k["gain"][pl.ds(128 * j, n)].reshape(1, n)
         col = jnp.sum(jnp.where(eye[:n, :n], row, 0.0), -1, keepdims=True)
         k["gc"][128 * j : 128 * j + n, :] = jnp.broadcast_to(col, (n, 128))
+    fetch["og"].wait()
     pl.semaphore_wait(barrier, len(PEERS))
 
     m_cp = []
@@ -169,20 +176,33 @@
         ])
     ag = [[] for _ in PLAN]
 
-    def gather(i, ds):
+    def lanes_of(a, d):
+        return pl.ds(pl.multiple_of(coord(a, d) * 128, 128), 128)
+
+    def gather(i):
         c0, nc, cw, a, p, q = PLAN[i]
         src = k["og"].at[pl.ds(c0, nc)]
-        dst = k[f"tok{i}"].at[pl.ds(0, nc), pl.ds(pl.multiple_of(me[a] * 128, 128), 128)]
-        for d in ds:
+        dst = k[f"tok{i}"].at[pl.ds(0, nc), lanes_of(a, 0)]
+        for n, d in enumerate((1, 3)):
+            ag[i].append(launch(src, dst, k["s_ag"].at[i, n], k["r_ag"].at[i, n], ring_offset(a, d)))
+
+    def relay(i):
+        c0, nc, cw, a, p, q = PLAN[i]
+        half = nc // 2
+        for n, d in enumerate((1, 3)):
+            ag[i][n].wait_recv()
+            piece = k[f"tok{i}"].at[pl.ds(n * half, half), lanes_of(a, 4 - d)]
             ag[i].append(
-                launch(src, dst, k["s_ag"].at[i, d - 1], k["r_ag"].at[i, d - 1], ring_offset(a, d))
+                launch(piece, piece, k["s_ag"].at[i, 2 + n], k["r_ag"].at[i, 2 + n], ring_offset(a, d))
             )
 
     for i in range(NCH):
-        gather(i, (2, 1, 3))
+        gather(i)
     for i, (c0, nc, cw, a, p, q) in enumerate(PLAN):
         k[f"tok{i}"][0:nc, pl.ds(pl.multiple_of(me[a] * 128, 128), 128)] = k["og"][c0 : c0 + nc, :]
 
+    fetch["res"].wait()
+    fetch["rw"].wait()
     floated = k["res"][...].astype(F32)
     inv = lax.rsqrt(jnp.mean(floated * floated, 0, keepdims=True) + 1e-05)
     normed = (floated * inv * k["gc"][...]).astype(BF)
@@ -211,7 +231,7 @@
                 marks = jnp.dot(k[f"pick{g}"][...], k[f"mg{g}"][s], preferred_element_type=F32)
                 hit = (marks == want) & (src_flat == s)
                 pb[:, s * 128 : (s + 1) * 128] = jnp.where(hit, 1.0, 0.0).astype(BF)
-        for cp in ag[i]:
+        for cp in ag[i][2:]:
             cp.wait_recv()
         rows = lax.dot_general(pb[...], k[f"tok{i}"][...], NT, preferred_element_type=F32)
         if i == LAST:
@@ -235,6 +255,12 @@
         b1[me[p]] = sel[tuple(me[p] if o == p else slice(None) for o in others)]
 
     for i in range(6):
+        relay(i)
+    for i in (0, 1, 2):
+        first_ring(i)
+    for i in (6, 7, 8):
+        relay(i)
+    for i in (3, 4, 5):
         first_ring(i)
 
     slot = lax.broadcasted_iota(jnp.int32, (768, 128), 0)
@@ -293,7 +319,7 @@
         k["rows"][:, c0 : c0 + nc] = rows.astype(BF)
         return weight
 
-    def inner_part(h):
+    def inner_part(h, first=0, last=FF // FB):
         cols = slice(PARTS[h], PARTS[h + 1])
 
         def step(n, carry):
@@ -305,7 +331,7 @@
                 k["acc"][at, :] += part
             return carry
 
-        lax.fori_loop(0, FF // FB, step, 0)
+        lax.fori_loop(first, last, step, 0)
 
     for i in (0, 1, 2):
         second_ring(i)
@@ -315,9 +341,10 @@
         second_ring(i)
     for i in (0, 1, 2):
         arrived(i)
-    inner_part(0)
+    inner_part(0, 0, 2)
     for i in (6, 7, 8):
         second_ring(i)
+    inner_part(0, 2, 3)
     for i in (3, 4, 5):
         arrived(i)
     inner_part(1)
@@ -347,15 +374,13 @@
 
     slot_score = jnp.sum(k["acc"][...] * k["hid"][...].astype(F32), 0, keepdims=True)
     hi = slot_score.astype(BF)
-    left = slot_score - hi.astype(F32)
-    mid = left.astype(BF)
-    lo = (left - mid.astype(F32)).astype(BF)
+    lo = (slot_score - hi.astype(F32)).astype(BF)
     g_row = lax.broadcasted_iota(jnp.int32, (128, 768), 0)
     g_lane = lax.broadcasted_iota(jnp.int32, (128, 768), 1)
     inside = (g_lane >= g_row * 6) & (g_lane < g_row * 6 + 6)
     place = jnp.where(rest == lane, 1.0, 0.0).astype(BF)
     packed = jnp.zeros((128, 128), F32)
-    for part in (hi, mid, lo):
+    for part in (hi, lo):
         spread_out = jnp.where(inside, part.astype(F32), 0.0).astype(BF)
         packed = packed + jnp.dot(spread_out, place, preferred_element_type=F32)
     k["rsc"][...] = packed.reshape(128, 1, 128)
@@ -414,6 +439,9 @@
             a1.append(launch(piece, k["ar1"].at[n, d - 1], k["s_a1"].at[n, d - 1], k["r_a1"].at[n, d - 1], ring_offset(a, d)))
     upper = normed_grad * k["gc"][...]
     k["rg"][...] = (inv * (upper - unit * jnp.mean(upper * unit, 0, keepdims=True))).astype(BF)
+    cp = pltpu.make_async_copy(k["rg"], k["rg_h"], k["loc"].at[12])
+    cp.start()
+    out_cps[5] = cp
     weight_grad(1)
 
     for n, (a, others) in enumerate(COLORS):
@@ -456,6 +484,9 @@
             g1.append(launch(piece, piece, k["s_g1"].at[n, d - 1], k["r_g1"].at[n, d - 1], ring_offset(a, d)))
     for cp in g1:
         cp.wait_recv()
+    cp = pltpu.make_async_copy(k["tot"], k["tot_h"], k["loc"].at[13])
+    cp.start()
+    out_cps[6] = cp
     for cp in pending:
         cp.wait_send()
     few = k["rsc"].at[pl.ds(0, 127)]
@@ -503,6 +534,8 @@
     hbm = pl.BlockSpec(memory_space=pl.ANY)
     dma = pltpu.SemaphoreType.DMA
     scratch = [
+        pltpu.VMEM((D, 128), BF), pltpu.VMEM((D, 128), BF), pltpu.VMEM((D,), F32), pltpu.VMEM((D, 128), BF),
+        pltpu.VMEM((4, 128), jnp.int32), pltpu.VMEM((D, 128), BF), pltpu.VMEM((384, 8, 128), BF),
         pltpu.VMEM((FF, 768), BF), pltpu.VMEM((FF, D), BF), pltpu.VMEM((FF, 768), F32), pltpu.VMEM((FF, 768), BF),
         pltpu.VMEM((128, 128), F32), pltpu.VMEM((128, 128), F32), pltpu.VMEM((D, 128), BF), pltpu.VMEM((D, 128), F32),
         pltpu.VMEM((128, 1, 128), F32), pltpu.VMEM((128, 1, 128), F32),
@@ -523,10 +556,10 @@
             pltpu.VMEM(sizes + (3, 8, cw), BF),
         ]
     ng = len(GDIMS)
-    scratch += [dma((ng, 3)), dma((ng, 3)), dma((3,)), dma((3,)), dma((NCH, 3)), dma((NCH, 3))]
+    scratch += [dma((ng, 3)), dma((ng, 3)), dma((3,)), dma((3,)), dma((NCH, 4)), dma((NCH, 4))]
     scratch += [dma((NCH, 3)), dma((NCH, 3)), dma((NCH, 7)), dma((NCH, 7))]
     scratch += [dma(()), dma(()), dma((3, 3)), dma((3, 3)), dma((3,)), dma((3,))]
-    scratch += [dma((3,)), dma((3,)), dma((3, 3)), dma((3, 3)), dma((7,))]
+    scratch += [dma((3,)), dma((3,)), dma((3, 3)), dma((3, 3)), dma((14,))]
     hidden_grad, weight_grad, residual_grad, total = pl.pallas_call(
         kernel,
         name="routed",
@@ -536,8 +569,8 @@
             jax.ShapeDtypeStruct((D, 128), BF),
             jax.ShapeDtypeStruct((384, 8, 128), BF),
         ),
-        in_specs=[vm, vm, vm, vm, vm, hbm, hbm],
-        out_specs=(hbm, hbm, vm, vm),
+        in_specs=[hbm] * 7,
+        out_specs=(hbm,) * 4,
         scratch_shapes=scratch,
         compiler_params=pltpu.CompilerParams(
             collective_id=0, has_side_effects=True, vmem_limit_bytes=67043328

time: 110 us -> 108 us (0.982)
  Pallas kernels: 109 us -> 107 us
    pallas_call x1, Pallas kernels: 99.5 us -> 96.6 us  [on_device(): pl.pallas_call(kernel, name='routed', out_shape=(jax.ShapeDtypeStruct((FF...]
where the time goes in v4:
time: 108 us; the launch traced here: 107 us
  Pallas kernels  107 us (99%)
    pallas_call x1, Pallas kernels, on_device(): pl.pallas_call(kernel, name='routed', out_shape=(jax.ShapeDtypeStruct((FF...  96.6 us
    pallas_call x1, Pallas kernels, on_device(): pl.pallas_call(finish, name='finish', out_shape=(jax.ShapeDtypeStruct((FF...  10 us

profile of v4, /device:TPU:1, one launch (start us, length us, event | category | flops | bytes accessed | tf_op | source)
XLA Modules:
  0.0 107.5 jit_solution(10615504154431846799)
XLA Ops:
  0.6 96.6 %routed.1 = (bf16[1440,768]{1,0:T(8,128)(2,1)}, bf16[1440,2880]{1,0:T(8,128)(2,1)}, bf16[2880,128]{1,0:T(8,128)(2,1)}, bf16[384,8,128]{2,1,0:T(8,128)(2,1)}) custom-call(bf16[2880,128]{1,0:T(8,128)(2,1)} %bitcast.14, bf16[2880,128]{1,0:T(8,128)(2,1)} %bitcast.15, f32[2880]{0:T(1024)} %refs_2_.1, bf16[2880,128]{1,0:T(8,128)(2,1)} %refs_3_.1, ...), custom_call_target="tpu_custom_call" | custom-call | tf_op jit(solution)/shard_map/routed/pallas_call | solution.py:563
  97.3 10.0 %finish.1 = (bf16[1440,768]{1,0:T(8,128)(2,1)}, bf16[1440,2880]{1,0:T(8,128)(2,1)}, bf16[2880,128]{1,0:T(8,128)(2,1)}, f32[2880,128]{1,0:T(8,128)}, f32[2880]{0:T(1024)}) custom-call(bf16[1440,768]{1,0:T(8,128)(2,1)} %get-tuple-element.14.hg, bf16[1440,2880]{1,0:T(8,128)(2,1)} %get-tuple-element.15.wg, bf16[2880,128]{1,0:T(8,128)(2,1)} %get-tuple-element.16.rg, ...), custom_call_target="tpu_custom_call" | custom-call | tf_op jit(solution)/shard_map/finish/pallas_call | solution.py:580

commit v5 on v4

--- a/solution.py
+++ b/solution.py
@@ -78,7 +78,7 @@
         ["og_h", "res_h", "gain_h", "rw_h", "ids_h", "hid_h", "w_h"]
         + ["hg_h", "wg_h", "rg_h", "tot_h"]
         + ["og", "res", "gain", "rw", "ids", "rg", "tot", "hid", "w", "acc", "hgs", "mt", "prob", "normedt", "gc"]
-        + ["rsc", "rr", "xs", "ar1", "as2", "ar2", "gv", "rows", "wgs0", "wgs1", "wgs3"]
+        + ["rsc", "rr", "xs", "ar1", "as2", "ar2", "gv", "rows", "wgs0", "wgs1", "wgs3", "idg"]
     )
     ng = len(GDIMS)
     names += [f"mg{g}" for g in range(ng)] + ["pg"] + [f"pb{g}" for g in range(ng)]
@@ -110,10 +110,10 @@
     pending = []
 
     def launch(src, dst, ssem, rsem, t):
-        cp = remote(src, dst, ssem, rsem, t)
-        cp.start()
-        pending.append(cp)
-        return cp
+        remote(src, dst, ssem, rsem, t).start()
+
+    def wait_all(ref, sem):
+        pltpu.make_async_copy(ref, ref, sem).wait()
 
     fetch = {}
     for n, name in enumerate(("ids", "gain", "og", "res", "rw")):
@@ -130,13 +130,17 @@
     e_row = lax.broadcasted_iota(jnp.int32, (128, 128), 0)
     t_col = lax.broadcasted_iota(jnp.int32, (128, 128), 1)
     fetch["ids"].wait()
-    match = e_row == k["ids"][0:1, :]
-    for j in range(1, 4):
-        match = match | (e_row == k["ids"][j : j + 1, :])
-    matchf = match.astype(F32)
     earlier = jnp.where(e_row < t_col, 1.0, 0.0).astype(BF)
-    count = jnp.dot(matchf.astype(BF), earlier, preferred_element_type=F32)
-    mt = matchf * (count + 1.0)
+
+    def marks_of(ids):
+        match = e_row == ids[0:1, :]
+        for j in range(1, 4):
+            match = match | (e_row == ids[j : j + 1, :])
+        ones = match.astype(F32)
+        count = jnp.dot(ones.astype(BF), earlier, preferred_element_type=F32)
+        return match, ones * (count + 1.0)
+
+    match, mt = marks_of(k["ids"][...])
     k["mt"][...] = mt
     for g, a in enumerate(GDIMS):
         k[f"mg{g}"][me[a]] = mt.astype(BF)
@@ -167,15 +171,10 @@
     fetch["og"].wait()
     pl.semaphore_wait(barrier, len(PEERS))
 
-    m_cp = []
     for g, a in enumerate(GDIMS):
-        own = k[f"mg{g}"].at[me[a]]
-        m_cp.append([
-            launch(own, own, k["s_m"].at[g, d - 1], k["r_m"].at[g, d - 1], ring_offset(a, d))
-            for d in (2, 1, 3)
-        ])
-    ag = [[] for _ in PLAN]
-
+        for d in (2, 1, 3):
+            launch(k["ids"], k["idg"].at[g, d - 1], k["s_m"], k["r_m"].at[g], ring_offset(a, d))
+    pending.append((k["idg"], k["s_m"]))
     def lanes_of(a, d):
         return pl.ds(pl.multiple_of(coord(a, d) * 128, 128), 128)
 
@@ -183,18 +182,18 @@
         c0, nc, cw, a, p, q = PLAN[i]
         src = k["og"].at[pl.ds(c0, nc)]
         dst = k[f"tok{i}"].at[pl.ds(0, nc), lanes_of(a, 0)]
-        for n, d in enumerate((1, 3)):
-            ag[i].append(launch(src, dst, k["s_ag"].at[i, n], k["r_ag"].at[i, n], ring_offset(a, d)))
+        for d in (1, 3):
+            launch(src, dst, k["s_ag"].at[i], k["r_ag"].at[i, 0], ring_offset(a, d))
 
     def relay(i):
         c0, nc, cw, a, p, q = PLAN[i]
         half = nc // 2
+        tok = k[f"tok{i}"]
+        wait_all(tok.at[pl.ds(0, nc), pl.ds(0, 256)], k["r_ag"].at[i, 0])
         for n, d in enumerate((1, 3)):
-            ag[i][n].wait_recv()
-            piece = k[f"tok{i}"].at[pl.ds(n * half, half), lanes_of(a, 4 - d)]
-            ag[i].append(
-                launch(piece, piece, k["s_ag"].at[i, 2 + n], k["r_ag"].at[i, 2 + n], ring_offset(a, d))
-            )
+            piece = tok.at[pl.ds(n * half, half), lanes_of(a, 4 - d)]
+            launch(piece, piece, k["s_ag"].at[i], k["r_ag"].at[i, 1], ring_offset(a, d))
+        pending.append((tok.at[pl.ds(0, nc), pl.ds(0, 384)], k["s_ag"].at[i]))
 
     for i in range(NCH):
         gather(i)
@@ -214,29 +213,28 @@
     pa = PLAN[LAST][3]
     k["pg"][me[pa]] = prob.astype(BF)
     own = k["pg"].at[me[pa]]
-    p_cp = [
-        launch(own, own, k["s_p"].at[d - 1], k["r_p"].at[d - 1], ring_offset(pa, d)) for d in (2, 1, 3)
-    ]
-
-    p1 = {}
+    for d in (2, 1, 3):
+        launch(own, own, k["s_p"], k["r_p"], ring_offset(pa, d))
+    pending.append((k["pg"].at[pl.ds(0, 3)], k["s_p"]))
+
+    for g, a in enumerate(GDIMS):
+        wait_all(k["idg"].at[g], k["r_m"].at[g])
+        for d in (1, 2, 3):
+            k[f"mg{g}"][coord(a, 4 - d)] = marks_of(k["idg"][g, d - 1])[1].astype(BF)
 
     def first_ring(i):
         c0, nc, cw, a, p, q = PLAN[i]
         g = GDIMS.index(a)
         pb = k[f"pb{g}"]
         if i < len(GDIMS):
-            for cp in m_cp[g]:
-                cp.wait_recv()
             for s in range(4):
                 marks = jnp.dot(k[f"pick{g}"][...], k[f"mg{g}"][s], preferred_element_type=F32)
                 hit = (marks == want) & (src_flat == s)
                 pb[:, s * 128 : (s + 1) * 128] = jnp.where(hit, 1.0, 0.0).astype(BF)
-        for cp in ag[i][2:]:
-            cp.wait_recv()
+        wait_all(k[f"tok{i}"].at[pl.ds(0, nc), pl.ds(0, 128)], k["r_ag"].at[i, 1])
         rows = lax.dot_general(pb[...], k[f"tok{i}"][...], NT, preferred_element_type=F32)
         if i == LAST:
-            for cp in p_cp:
-                cp.wait_recv()
+            wait_all(k["pg"].at[pl.ds(0, 3)], k["r_p"])
             sent = jnp.zeros((768, 128), F32)
             for s in range(4):
                 weights = jnp.dot(k[f"pick{g}"][...], k["pg"][s], preferred_element_type=F32)
@@ -247,11 +245,10 @@
         others = OTHER[a]
         sel, b1 = k[f"sel{i}"], k[f"b1_{i}"]
         sel[...] = rows.reshape(tuple(SZ[o] for o in others) + (3, 8, cw)).astype(BF)
-        cps = []
         for d in (2, 1, 3):
             spot = tuple(coord(p, d) if o == p else slice(None) for o in others)
-            cps.append(launch(sel.at[spot], b1.at[me[p]], k["s_p1"].at[i, d - 1], k["r_p1"].at[i, d - 1], ring_offset(p, d)))
-        p1[i] = cps
+            launch(sel.at[spot], b1.at[me[p]], k["s_p1"].at[i], k["r_p1"].at[i], ring_offset(p, d))
+        pending.append((b1.at[pl.ds(0, 3)], k["s_p1"].at[i]))
         b1[me[p]] = sel[tuple(me[p] if o == p else slice(None) for o in others)]
 
     for i in range(6):
@@ -275,12 +272,9 @@
     w_copy.wait()
     hid_copy.wait()
 
-    p2 = {}
-
     def second_ring(i):
         c0, nc, cw, a, p, q = PLAN[i]
-        for cp in p1[i]:
-            cp.wait_recv()
+        wait_all(k[f"b1_{i}"].at[pl.ds(0, 3)], k["r_p1"].at[i])
         others = OTHER[a]
         left = tuple(o for o in others if o != p)
         spot = tuple(slice(None) if o == p else me[o] for o in others)
@@ -289,23 +283,19 @@
         def part_of(dq, dc):
             return (slice(None),) + tuple(coord(q, dq) if o == q else coord(CORE, dc) for o in left)
 
-        cps = []
-        n = 0
         for dq in (2, 1, 3, 0):
             for dc in (0, 1):
                 if dq == 0 and dc == 0:
                     continue
                 t = [0, 0, 0, 0]
                 t[q], t[CORE] = dq, dc
-                cps.append(launch(b1.at[part_of(dq, dc)], fin.at[spot], k["s_p2"].at[i, n], k["r_p2"].at[i, n], tuple(t)))
-                n += 1
-        p2[i] = cps
+                launch(b1.at[part_of(dq, dc)], fin.at[spot], k["s_p2"].at[i], k["r_p2"].at[i], tuple(t))
+        pending.append((k["rows"].at[pl.ds(0, 672), pl.ds(0, cw)], k["s_p2"].at[i]))
         fin[spot] = b1[part_of(0, 0)]
 
     def arrived(i):
         c0, nc, cw, a, p, q = PLAN[i]
-        for cp in p2[i]:
-            cp.wait_recv()
+        wait_all(k["rows"].at[pl.ds(0, 672), pl.ds(0, cw)], k["r_p2"].at[i])
         rows = k[f"fin{i}"][...].reshape(96, 8, cw).astype(F32).reshape(768, cw)
         if a != Y:
             rows = jnp.dot(k[f"perm{a}"][...], rows.astype(BF), preferred_element_type=F32)
@@ -411,9 +401,26 @@
         return top, (v - top.astype(F32)).astype(BF)
 
     hi, lo = halves(grad)
-    local = jnp.dot(k["normedt"][...], hi, preferred_element_type=F32) + jnp.dot(
-        k["normedt"][...], lo, preferred_element_type=F32
-    )
+    xs = k["xs"]
+    def router_rows(n):
+        at = slice(1024 * n, min(D, 1024 * n + 1024))
+        local = jnp.dot(k["normedt"][at, :], hi, preferred_element_type=F32) + jnp.dot(
+            k["normedt"][at, :], lo, preferred_element_type=F32
+        )
+        blocks = (at.stop - at.start) // 8
+        xs[pl.ds(128 * n, blocks)] = local.reshape(blocks, 8, 128).astype(BF)
+
+    def send_color(n):
+        a = COLORS[n][0]
+        for d in (2, 1, 3):
+            piece = xs.at[pl.ds(pl.multiple_of(128 * n + 32 * coord(a, d), 32), 32)]
+            launch(piece, k["ar1"].at[n, d - 1], k["s_a1"].at[n], k["r_a1"].at[n], ring_offset(a, d))
+        pending.append((k["ar1"].at[n], k["s_a1"].at[n]))
+
+    for n in range(2):
+        router_rows(n)
+        send_color(n)
+    router_rows(2)
     hi, lo = halves(grad_t)
     normed_grad = jnp.dot(k["rw"][...], hi, preferred_element_type=F32) + jnp.dot(
         k["rw"][...], lo, preferred_element_type=F32
@@ -427,16 +434,9 @@
         n = min(128, D - 128 * j)
         col = gain_col[128 * j : 128 * j + n]
         k["gv"][j : j + 1, 0:n] = jnp.sum(jnp.where(eye[:n, :n], col, 0.0), 0, keepdims=True)
-    xs = k["xs"]
-    xs[pl.ds(0, 360)] = local.reshape(360, 8, 128).astype(BF)
     xs[pl.ds(360, 3)] = k["gv"][...].reshape(3, 8, 128).astype(BF)
     xs[pl.ds(363, 21)] = jnp.zeros((21, 8, 128), BF)
-
-    a1 = []
-    for n, (a, others) in enumerate(COLORS):
-        for d in (2, 1, 3):
-            piece = xs.at[pl.ds(pl.multiple_of(128 * n + 32 * coord(a, d), 32), 32)]
-            a1.append(launch(piece, k["ar1"].at[n, d - 1], k["s_a1"].at[n, d - 1], k["r_a1"].at[n, d - 1], ring_offset(a, d)))
+    send_color(2)
     upper = normed_grad * k["gc"][...]
     k["rg"][...] = (inv * (upper - unit * jnp.mean(upper * unit, 0, keepdims=True))).astype(BF)
     cp = pltpu.make_async_copy(k["rg"], k["rg_h"], k["loc"].at[12])
@@ -445,8 +445,7 @@
     weight_grad(1)
 
     for n, (a, others) in enumerate(COLORS):
-        for cp in a1[3 * n : 3 * n + 3]:
-            cp.wait_recv()
+        wait_all(k["ar1"].at[n], k["r_a1"].at[n])
         total = xs[pl.ds(pl.multiple_of(128 * n + 32 * me[a], 32), 32)].astype(F32)
         for d in range(3):
             total = total + k["ar1"][n, d].astype(F32)
@@ -475,20 +474,21 @@
             cp = remote(tot.at[at], tot.at[at], k["s_g2"].at[n], k["r_g2"].at[n], t)
             cp.start()
     weight_grad(3)
-    g1 = []
     for n, (a, others) in enumerate(COLORS):
         few = k["as2"].at[n, pl.ds(0, 31)]
         pltpu.make_async_copy(few, few, k["r_g2"].at[n]).wait()
         piece = tot.at[pl.ds(pl.multiple_of(128 * n + 32 * me[a], 32), 32)]
         for d in (2, 1, 3):
-            g1.append(launch(piece, piece, k["s_g1"].at[n, d - 1], k["r_g1"].at[n, d - 1], ring_offset(a, d)))
-    for cp in g1:
-        cp.wait_recv()
-    cp = pltpu.make_async_copy(k["tot"], k["tot_h"], k["loc"].at[13])
-    cp.start()
-    out_cps[6] = cp
-    for cp in pending:
-        cp.wait_send()
+            launch(piece, piece, k["s_g1"].at[n], k["r_g1"].at[n], ring_offset(a, d))
+        pending.append((tot.at[pl.ds(0, 96)], k["s_g1"].at[n]))
+    for n in range(3):
+        wait_all(tot.at[pl.ds(0, 96)], k["r_g1"].at[n])
+        blocks = pl.ds(128 * n, 128)
+        cp = pltpu.make_async_copy(k["tot"].at[blocks], k["tot_h"].at[blocks], k["loc"].at[13 + n])
+        cp.start()
+        out_cps[6 + n] = cp
+    for ref, sem in pending:
+        wait_all(ref, sem)
     few = k["rsc"].at[pl.ds(0, 127)]
     pltpu.make_async_copy(few, few, k["s_ret"]).wait()
     for n in range(3):
@@ -542,6 +542,7 @@
         pltpu.VMEM((384, 8, 128), BF), pltpu.VMEM((3, 3, 32, 8, 128), BF), pltpu.VMEM((3, 32, 8, 128), BF),
         pltpu.VMEM((3, 32, 8, 128), BF), pltpu.VMEM((24, 128), F32), pltpu.VMEM((768, D), BF),
         pltpu.VMEM((FF, 768), BF), pltpu.VMEM((FF, 768), BF), pltpu.VMEM((FF, 576), BF),
+        pltpu.VMEM((3, 3, 4, 128), jnp.int32),
     ]
     scratch += [pltpu.VMEM((4, 128, 128), BF) for _ in GDIMS]
     scratch += [pltpu.VMEM((4, 128, 128), BF)]
@@ -555,11 +556,10 @@
             pltpu.VMEM((4,) + tuple(SZ[o] for o in OTHER[a] if o != p) + (3, 8, cw), BF),
             pltpu.VMEM(sizes + (3, 8, cw), BF),
         ]
-    ng = len(GDIMS)
-    scratch += [dma((ng, 3)), dma((ng, 3)), dma((3,)), dma((3,)), dma((NCH, 4)), dma((NCH, 4))]
-    scratch += [dma((NCH, 3)), dma((NCH, 3)), dma((NCH, 7)), dma((NCH, 7))]
-    scratch += [dma(()), dma(()), dma((3, 3)), dma((3, 3)), dma((3,)), dma((3,))]
-    scratch += [dma((3,)), dma((3,)), dma((3, 3)), dma((3, 3)), dma((14,))]
+    scratch += [dma(()), dma((3,)), dma(()), dma(()), dma((NCH,)), dma((NCH, 2))]
+    scratch += [dma((NCH,)), dma((NCH,)), dma((NCH,)), dma((NCH,))]
+    scratch += [dma(()), dma(()), dma((3,)), dma((3,)), dma((3,)), dma((3,))]
+    scratch += [dma((3,)), dma((3,)), dma((3,)), dma((3,)), dma((16,))]
     hidden_grad, weight_grad, residual_grad, total = pl.pallas_call(
         kernel,
         name="routed",

time: 108 us -> 104 us (0.963)
  Pallas kernels: 107 us -> 103 us
    pallas_call x1, Pallas kernels: 96.6 us -> 92.8 us  [on_device(): pl.pallas_call(kernel, name='routed', out_shape=(jax.ShapeDtypeStruct((FF...]
where the time goes in v5:
time: 104 us
  Pallas kernels  103 us (99%)
    pallas_call x1, Pallas kernels, on_device(): pl.pallas_call(kernel, name='routed', out_shape=(jax.ShapeDtypeStruct((FF...  92.8 us
    pallas_call x1, Pallas kernels, on_device(): pl.pallas_call(finish, name='finish', out_shape=(jax.ShapeDtypeStruct((FF...  10 us

profile of v5, /device:TPU:1, one launch (start us, length us, event | category | flops | bytes accessed | tf_op | source)
XLA Modules:
  0.0 103.6 jit_solution(3044174847536113979)
XLA Ops:
  0.6 92.8 %routed.1 = (bf16[1440,768]{1,0:T(8,128)(2,1)}, bf16[1440,2880]{1,0:T(8,128)(2,1)}, bf16[2880,128]{1,0:T(8,128)(2,1)}, bf16[384,8,128]{2,1,0:T(8,128)(2,1)}) custom-call(bf16[2880,128]{1,0:T(8,128)(2,1)} %bitcast.14, bf16[2880,128]{1,0:T(8,128)(2,1)} %bitcast.15, f32[2880]{0:T(1024)} %refs_2_.1, bf16[2880,128]{1,0:T(8,128)(2,1)} %refs_3_.1, ...), custom_call_target="tpu_custom_call" | custom-call | tf_op jit(solution)/shard_map/routed/pallas_call | solution.py:563
  93.4 10.0 %finish.1 = (bf16[1440,768]{1,0:T(8,128)(2,1)}, bf16[1440,2880]{1,0:T(8,128)(2,1)}, bf16[2880,128]{1,0:T(8,128)(2,1)}, f32[2880,128]{1,0:T(8,128)}, f32[2880]{0:T(1024)}) custom-call(bf16[1440,768]{1,0:T(8,128)(2,1)} %get-tuple-element.14.hg, bf16[1440,2880]{1,0:T(8,128)(2,1)} %get-tuple-element.15.wg, bf16[2880,128]{1,0:T(8,128)(2,1)} %get-tuple-element.16.rg, ...), custom_call_target="tpu_custom_call" | custom-call | tf_op jit(solution)/shard_map/finish/pallas_call | solution.py:580

commit v6 on v5

--- a/solution.py
+++ b/solution.py
@@ -226,11 +226,6 @@
         c0, nc, cw, a, p, q = PLAN[i]
         g = GDIMS.index(a)
         pb = k[f"pb{g}"]
-        if i < len(GDIMS):
-            for s in range(4):
-                marks = jnp.dot(k[f"pick{g}"][...], k[f"mg{g}"][s], preferred_element_type=F32)
-                hit = (marks == want) & (src_flat == s)
-                pb[:, s * 128 : (s + 1) * 128] = jnp.where(hit, 1.0, 0.0).astype(BF)
         wait_all(k[f"tok{i}"].at[pl.ds(0, nc), pl.ds(0, 128)], k["r_ag"].at[i, 1])
         rows = lax.dot_general(pb[...], k[f"tok{i}"][...], NT, preferred_element_type=F32)
         if i == LAST:
@@ -251,7 +246,14 @@
         pending.append((b1.at[pl.ds(0, 3)], k["s_p1"].at[i]))
         b1[me[p]] = sel[tuple(me[p] if o == p else slice(None) for o in others)]
 
-    for i in range(6):
+    for i in range(3):
+        relay(i)
+    for g in range(len(GDIMS)):
+        for s in range(4):
+            marks = jnp.dot(k[f"pick{g}"][...], k[f"mg{g}"][s], preferred_element_type=F32)
+            hit = (marks == want) & (src_flat == s)
+            k[f"pb{g}"][:, s * 128 : (s + 1) * 128] = jnp.where(hit, 1.0, 0.0).astype(BF)
+    for i in range(3, 6):
         relay(i)
     for i in (0, 1, 2):
         first_ring(i)

time: 104 us -> 103 us (level)
  no operation moved by 1% of the time
where the time goes in v6:
time: 103 us
  Pallas kernels  102 us (99%)
    pallas_call x1, Pallas kernels, on_device(): pl.pallas_call(kernel, name='routed', out_shape=(jax.ShapeDtypeStruct((FF...  92.4 us
    pallas_call x1, Pallas kernels, on_device(): pl.pallas_call(finish, name='finish', out_shape=(jax.ShapeDtypeStruct((FF...  10 us

profile of v6, /device:TPU:1, one launch (start us, length us, event | category | flops | bytes accessed | tf_op | source)
XLA Modules:
  0.0 103.3 jit_solution(9791463314312786838)
XLA Ops:
  0.6 92.4 %routed.1 = (bf16[1440,768]{1,0:T(8,128)(2,1)}, bf16[1440,2880]{1,0:T(8,128)(2,1)}, bf16[2880,128]{1,0:T(8,128)(2,1)}, bf16[384,8,128]{2,1,0:T(8,128)(2,1)}) custom-call(bf16[2880,128]{1,0:T(8,128)(2,1)} %bitcast.14, bf16[2880,128]{1,0:T(8,128)(2,1)} %bitcast.15, f32[2880]{0:T(1024)} %refs_2_.1, bf16[2880,128]{1,0:T(8,128)(2,1)} %refs_3_.1, ...), custom_call_target="tpu_custom_call" | custom-call | tf_op jit(solution)/shard_map/routed/pallas_call | solution.py:565
  93.1 10.0 %finish.1 = (bf16[1440,768]{1,0:T(8,128)(2,1)}, bf16[1440,2880]{1,0:T(8,128)(2,1)}, bf16[2880,128]{1,0:T(8,128)(2,1)}, f32[2880,128]{1,0:T(8,128)}, f32[2880]{0:T(1024)}) custom-call(bf16[1440,768]{1,0:T(8,128)(2,1)} %get-tuple-element.14.hg, bf16[1440,2880]{1,0:T(8,128)(2,1)} %get-tuple-element.15.wg, bf16[2880,128]{1,0:T(8,128)(2,1)} %get-tuple-element.16.rg, ...), custom_call_target="tpu_custom_call" | custom-call | tf_op jit(solution)/shard_map/finish/pallas_call | solution.py:582
